TPU v7x, 1024 devices: a whole 4x8x16 slice. The times are simulated.
1024 devices in a mesh: group: 16 (over y, x_hi), expert: 32 (over z, core), dp: 2 (over x_lo).
Axes of the slice: x: 4 (x_hi: 2, x_lo: 2; x = x_hi * 2 + x_lo), y: 8, z: 16, core: 2. Of those that a mesh axis runs over, the one named last changes fastest.
Arguments:
- tokens: bfloat16 [64, 64, 7168], P(('expert', 'dp'), 'group'), may hold values from -6 to 6
- expert_ids: int32 [64, 64, 8], P(('expert', 'dp')), may hold values from 0 to 255, as said below
- gate_codes: int32 [64, 64, 8], P(('expert', 'dp')), may hold values from 1 to 1023
- w_gate: bfloat16 [32, 7168, 2048], P('expert', None, 'group'), may hold values from -0.0625 to 0.0625
- w_up: bfloat16 [32, 7168, 2048], P('expert', None, 'group'), may hold values from -0.0625 to 0.0625
- w_down: bfloat16 [32, 2048, 7168], P('expert', 'group'), may hold values from -0.125 to 0.125
Outputs:
- mixed: bfloat16 [64, 64, 7168], P(('expert', 'dp'), 'group')
Inputs may be any that keep to these rules, and one draw needn't show every extreme that they name: `expert_ids`: each token names 8 different experts, all within at most 4 of the 8 groups of 32 consecutive ids. In every set (one index of the first dimension), each expert below 32 is named by at most 4 tokens, and some expert by exactly 4; a token names at most 4 experts below 32.
All inputs are finite; a program needn't handle non-finite values.
Results may differ from a plain program's by a relative error of at most 0.015.
Values may be sent and summed in bfloat16 or wider, within the bound.
No kernel may reach another device: no remote copies, remote signals or barrier semaphores. Data moves between devices by JAX's collectives and lax.ppermute only.
A program may use at most 64 MiB of HBM per device.

v0:
```python
import jax
import jax.numpy as jnp
from jax import lax
from jax.experimental import pallas as pl
from jax.experimental.pallas import tpu as pltpu
from jax.sharding import Mesh
from jax.sharding import PartitionSpec as P


CAPG = 4
GROUP = ("y", "xh")
EXPERT = ("z", "core")
SETS_OVER = ("z", "core", "dp")


def exchange(parts, axes):
    return lax.all_to_all(parts, axes, 0, 0, tiled=True)


SMALL = pltpu.CompilerParams(vmem_limit_bytes=8 * 2**20)


def vmem():
    return pl.BlockSpec(memory_space=pltpu.VMEM)


def in_vmem(x):
    return pltpu.with_memory_space_constraint(x, pltpu.VMEM)


def anywhere():
    return pl.BlockSpec(memory_space=pl.ANY)


def in_columns(rows, pieces, copies):
    own, width = rows.shape
    cols = width // pieces

    def kernel(rows_ref, out_ref):
        for i in range(pieces):
            piece = rows_ref[:, i * cols : (i + 1) * cols]
            for j in range(copies):
                out_ref[i * copies + j] = piece

    return pl.pallas_call(
        kernel,
        out_shape=jax.ShapeDtypeStruct((pieces * copies, own, cols), rows.dtype),
        in_specs=[vmem()],
        out_specs=vmem(),
        name="in_columns",
        compiler_params=SMALL,
    )(rows)


def signed(k):
    here, side = lax.axis_index("y"), lax.axis_index("dp")
    away = 1 - 2 * side if k < 3 else 2 * side - 1
    return here, side, away * k


def cut_blocks(matrix):
    n, far = lax.axis_size("y"), lax.axis_size("y") // 2
    rows, width = matrix.shape
    cols, half = width // n, rows // 2

    def kernel(matrix_ref, *refs):
        outs, sems = refs[: far + 1], refs[far + 1]
        copies = []
        for k in range(far + 1):
            here, side, step = signed(k)
            step = far if k == far else step
            at = pl.multiple_of(lax.rem(here + step + n, n) * cols, cols)
            lines = pl.ds(pl.multiple_of(side * half, half), half) if k == far else slice(None)
            source = matrix_ref.at[lines, pl.ds(at, cols)]
            copies.append(pltpu.make_async_copy(source, outs[k], sems.at[k]))
        for copy in copies:
            copy.start()
        for copy in copies:
            copy.wait()

    whole, part = pltpu.VMEM((rows, cols), matrix.dtype), pltpu.VMEM((half, cols), matrix.dtype)
    return pl.pallas_call(
        kernel,
        out_shape=[whole] * far + [part],
        in_specs=[anywhere()],
        out_specs=[vmem()] * (far + 1),
        scratch_shapes=[pltpu.SemaphoreType.DMA((far + 1,))],
        name="cut_blocks",
        compiler_params=SMALL,
    )(pltpu.with_memory_space_constraint(matrix, pltpu.HBM))


def stacked(parts):
    counts = [p.shape[0] for p in parts]

    def kernel(*refs):
        at = 0
        for ref, count in zip(refs, counts):
            refs[-1][at : at + count, :] = ref[...]
            at += count

    return pl.pallas_call(
        kernel,
        out_shape=pltpu.VMEM((sum(counts), parts[0].shape[1]), parts[0].dtype),
        in_specs=[vmem()] * len(parts),
        out_specs=vmem(),
        name="stacked",
        compiler_params=SMALL,
    )(*parts)


def down_product(hiddens, own, mine, others):
    n, far = lax.axis_size("y"), lax.axis_size("y") // 2
    rows, hid = hiddens.shape[1:]
    half, cols = hid // 2, own.shape[1]

    def kernel(hid_ref, own_ref, mine_ref, others_ref, outs_ref, far_ref):
        here, side, _ = signed(1)
        total = jnp.dot(hid_ref[here], own_ref[...], preferred_element_type=jnp.float32)
        for k in range(1, far):
            _, _, step = signed(k)
            lines = slice((k - 1) * hid, k * hid)
            for sign, ref in ((1, mine_ref), (-1, others_ref)):
                part = hid_ref[lax.rem(here - sign * step + n, n)]
                total += jnp.dot(part, ref[lines, :], preferred_element_type=jnp.float32)
        lines = slice((far - 1) * hid, (far - 1) * hid + half)
        far_ref[pl.ds(pl.multiple_of(side * half, half), half), :] = mine_ref[lines, :]
        far_ref[pl.ds(pl.multiple_of((1 - side) * half, half), half), :] = others_ref[lines, :]
        part = hid_ref[lax.rem(here + far, n)]
        total += jnp.dot(part, far_ref[...], preferred_element_type=jnp.float32)
        outs_ref[...] = total.astype(outs_ref.dtype)

    return pl.pallas_call(
        kernel,
        out_shape=jax.ShapeDtypeStruct((rows, cols), jnp.bfloat16),
        in_specs=[vmem()] * 4,
        out_specs=vmem(),
        scratch_shapes=[pltpu.VMEM((hid, cols), own.dtype)],
        name="down_product",
        compiler_params=SMALL,
    )(*(in_vmem(x) for x in (hiddens, own, mine, others)))


def gate_up_step(sums, shard, gate, up, step, axis):
    n = lax.axis_size(axis)
    rows, cols = shard.shape
    hid = gate.shape[1]
    first = sums is None

    def kernel(*refs):
        shard_ref, gate_ref, up_ref = refs[:3]
        here = lax.axis_index(axis)
        at = pl.multiple_of(lax.rem(here + step + n, n) * cols, cols)
        block = shard_ref[...]
        for i, weight in enumerate((gate_ref, up_ref)):
            got = jnp.dot(block, weight[pl.ds(at, cols), :], preferred_element_type=jnp.float32)
            refs[-2 + i][...] = got if first else refs[3 + i][...] + got

    return pl.pallas_call(
        kernel,
        out_shape=[pltpu.VMEM((rows, hid), jnp.float32)] * 2,
        in_specs=[vmem()] * (3 if first else 5),
        out_specs=[vmem()] * 2,
        name="gate_up_step",
        compiler_params=SMALL,
    )(*(in_vmem(x) for x in (shard, gate, up, *(sums or ()))))


def routing(expert_ids, gate_codes, experts, capacity):
    window = jnp.arange(experts, dtype=jnp.int32)
    hits = expert_ids[..., None] == window
    member = jnp.any(hits, axis=-2)
    codes = gate_codes.astype(jnp.float32)
    gates = 2.5 * codes / jnp.sum(codes, axis=-1, keepdims=True)
    weight = jnp.sum(jnp.where(hits, gates[..., None], jnp.float32(0.0)), axis=-2)
    tokens = expert_ids.shape[0]
    before = jnp.tril(jnp.ones((tokens, tokens), jnp.bfloat16), -1)
    rank = jnp.dot(before, member.astype(jnp.bfloat16), preferred_element_type=jnp.float32)
    slots = jnp.arange(capacity, dtype=jnp.float32)
    place = member[..., None] & (rank[..., None] == slots)
    return place, weight


def around(shard, axis):
    n = lax.axis_size(axis)
    up = [(i, (i + 1) % n) for i in range(n)]
    down = [(i, (i - 1) % n) for i in range(n)]
    found = [(0, shard)]
    a = b = shard
    for k in range(1, n // 2 + 1):
        a = lax.ppermute(a, axis, up)
        found.append((-k, a))
        if 2 * k < n:
            b = lax.ppermute(b, axis, down)
            found.append((k, b))
    return found


def per_device(tokens, expert_ids, gate_codes, w_gate, w_up, w_down):
    ny, nh = lax.axis_size("y"), lax.axis_size("xh")
    experts = lax.axis_size(EXPERT)
    own, width = tokens.shape[1], tokens.shape[2]
    cols = width // ny
    hid = w_gate.shape[2]

    toks = exchange(in_columns(tokens[0], ny, nh), GROUP)
    own_block, *blocks = cut_blocks(w_down[0])
    sides = lax.axis_size("dp")
    for k in range(1, ny // 2 + 1):
        pairs = []
        for i in range(ny):
            for side in range(sides):
                away = k if (side == 0) == (k != 3) else -k
                pairs.append((i * sides + side, (i + away) % ny * sides + side))
        blocks[k - 1] = lax.ppermute(blocks[k - 1], ("y", "dp"), pairs)
    mine = stacked(blocks)
    others = lax.ppermute(mine, "dp", [(0, 1), (1, 0)])

    place, weight = routing(expert_ids[0], gate_codes[0], experts, CAPG)
    mix = jnp.where(place, weight[..., None], jnp.float32(0.0))
    rows = jnp.einsum(
        "tej,td->ejd",
        place.astype(jnp.bfloat16),
        toks.reshape(ny * nh * own, cols),
        preferred_element_type=jnp.float32,
    ).astype(jnp.bfloat16)
    got = exchange(rows, EXPERT)
    sets = got.shape[0]
    count = sets * CAPG
    sums = None
    for step, shard in around(got.reshape(count, cols), "y"):
        sums = gate_up_step(sums, shard, w_gate[0], w_up[0], step, "y")
    first, second = sums
    hidden = (jax.nn.silu(first) * second).astype(jnp.bfloat16)
    hiddens = exchange(jnp.broadcast_to(hidden[None], (ny, count, hid)), "y")
    outs = down_product(hiddens, own_block, mine, others)
    back = exchange(outs.reshape(sets, CAPG, cols), EXPERT)
    mixed = jnp.einsum(
        "tej,ejc->tc",
        mix,
        back.astype(jnp.float32),
        precision=lax.Precision.HIGHEST,
        preferred_element_type=jnp.float32,
    )
    home = exchange(mixed.astype(jnp.bfloat16).reshape(ny * nh, own, cols), GROUP)
    home = home.reshape(ny, nh, own, cols).astype(jnp.float32)
    home = jnp.sum(home, axis=1).astype(jnp.bfloat16)
    return jnp.concatenate([home[i] for i in range(ny)], axis=1)[None]


def solution(mesh):
    fine = Mesh(
        mesh.devices.reshape(8, 2, 16, 2, mesh.shape["dp"]), ("y", "xh", "z", "core", "dp")
    )
    placed = (
        P(SETS_OVER, GROUP, None),
        P(SETS_OVER, None, None),
        P(SETS_OVER, None, None),
        P(EXPERT, None, GROUP),
        P(EXPERT, None, GROUP),
        P(EXPERT, GROUP, None),
    )
    return jax.shard_map(
        per_device,
        mesh=fine,
        in_specs=placed,
        out_specs=P(SETS_OVER, GROUP, None),
        check_vma=False,
    )
```

profile of v0, /device:TPU:2, one launch (start us, length us, event | category | flops | bytes accessed | tf_op | source)
XLA Modules:
  0.0 179.8 jit_solution(2763446253677921749)
XLA Ops:
  0.0 0.8 copy-done.2
  0.8 0.7 in_columns.1
  1.5 8.8 %all-to-all-start = ((bf16[16,4,896]{2,1,0:T(4,128)(2,1)}), bf16[16,4,896]{2,1,0:T(4,128)(2,1)S(1)}, u32[]{:S(2)}, u32[]{:S(2)}) async-start(bf16[16,4,896]{2,1,0:T(4,128)(2,1)} %in_columns.1), calls=%async_computation | async-start | bytes 229376 | tf_op jit(solution)/shard_map/all_to_all | solution.py:17
  10.3 0.7 fusion.2
  11.0 0.2 fusion.14
  11.2 10.1 %all-to-all-done = bf16[16,4,896]{2,1,0:T(4,128)(2,1)S(1)} async-done(((bf16[16,4,896]{2,1,0:T(4,128)(2,1)}), bf16[16,4,896]{2,1,0:T(4,128)(2,1)S(1)}, u32[]{:S(2)}, u32[]{:S(2)}) %all-to-all-start) | async-done | bytes 114720 | tf_op jit(solution)/shard_map/all_to_all | solution.py:17
  21.3 0.2 convolution_convert_fusion
  21.5 0.1 copy.15
  21.6 40.4 %all_to_all.25 = bf16[32,4,896]{2,1,0:T(4,128)(2,1)S(1)} all-to-all(bf16[32,4,896]{2,1,0:T(4,128)(2,1)S(1)} %copy.15), channel_id=1, replica_groups=mesh['y'=8,'xh'=2,'z'=16,'core'=2,'dp'=2] {'z','core'}, dimensions={0} | all-to-all | bytes 458752 | tf_op jit(solution)/shard_map/all_to_all | solution.py:17
  61.9 0.1 reshape.46.refs_0_
  62.0 2.6 %collective-permute-start = (bf16[128,896]{1,0:T(8,128)(2,1)S(1)}, bf16[128,896]{1,0:T(8,128)(2,1)S(1)}, u32[]{:S(2)}, u32[]{:S(2)}) collective-permute-start(bf16[128,896]{1,0:T(8,128)(2,1)S(1)} %reshape.46.refs_0_), channel_id=1, source_target_pairs={{0,128},{128,256},{256,384},{384,512},{512,640},{640,768},{768,896... | collective-permute-start | bytes 688136 | tf_op jit(solution)/shard_map/ppermute | solution.py:191
  64.6 4.7 %collective-permute-start.4 = (bf16[128,896]{1,0:T(8,128)(2,1)S(1)}, bf16[128,896]{1,0:T(8,128)(2,1)S(1)}, u32[]{:S(2)}, u32[]{:S(2)}) collective-permute-start(bf16[128,896]{1,0:T(8,128)(2,1)S(1)} %reshape.46.refs_0_), channel_id=1, source_target_pairs={{0,896},{128,0},{256,128},{384,256},{512,384},{640,512},{768,640},... | collective-permute-start | bytes 688136 | tf_op jit(solution)/shard_map/ppermute | solution.py:194
  69.4 2.7 %collective-permute-done.refs_0_ = bf16[128,896]{1,0:T(8,128)(2,1)S(1)} collective-permute-done((bf16[128,896]{1,0:T(8,128)(2,1)S(1)}, bf16[128,896]{1,0:T(8,128)(2,1)S(1)}, u32[]{:S(2)}, u32[]{:S(2)}) %collective-permute-start) | collective-permute-done | bytes 229408 | tf_op jit(solution)/shard_map/ppermute | solution.py:191
  72.1 1.9 %collective-permute-start.1 = (bf16[128,896]{1,0:T(8,128)(2,1)S(1)}, bf16[128,896]{1,0:T(8,128)(2,1)S(1)}, u32[]{:S(2)}, u32[]{:S(2)}) collective-permute-start(bf16[128,896]{1,0:T(8,128)(2,1)S(1)} %collective-permute-done.refs_0_), channel_id=1, source_target_pairs={{0,128},{128,256},{256,384},{384,512},{512,640},{640,768},{768,896... | collective-permute-start | bytes 688136 | tf_op jit(solution)/shard_map/ppermute | solution.py:191
  74.0 1.4 cut_blocks.1
  75.4 2.8 %collective-permute-start.10 = (bf16[64,896]{1,0:T(8,128)(2,1)S(1)}, bf16[64,896]{1,0:T(8,128)(2,1)S(1)}, u32[]{:S(2)}, u32[]{:S(2)}) collective-permute-start(bf16[64,896]{1,0:T(8,128)(2,1)S(1)} %get-tuple-element.46), channel_id=1, source_target_pairs={{0,512},{1,513},{128,640},{129,641},{256,768},{257,769},{384,896},... | collective-permute-start | bytes 344072 | tf_op jit(solution)/shard_map/ppermute | solution.py:215
  78.2 5.0 %collective-permute-start.5 = (bf16[128,896]{1,0:T(8,128)(2,1)S(1)}, bf16[128,896]{1,0:T(8,128)(2,1)S(1)}, u32[]{:S(2)}, u32[]{:S(2)}) collective-permute-start(bf16[128,896]{1,0:T(8,128)(2,1)S(1)} %collective-permute-done.4.refs_0_), channel_id=1, source_target_pairs={{0,896},{128,0},{256,128},{384,256},{512,384},{640,512},{768,640},... | collective-permute-start | bytes 688136 | tf_op jit(solution)/shard_map/ppermute | solution.py:194
  83.2 2.2 %collective-permute-done.1.refs_0_ = bf16[128,896]{1,0:T(8,128)(2,1)S(1)} collective-permute-done((bf16[128,896]{1,0:T(8,128)(2,1)S(1)}, bf16[128,896]{1,0:T(8,128)(2,1)S(1)}, u32[]{:S(2)}, u32[]{:S(2)}) %collective-permute-start.1) | collective-permute-done | bytes 229408 | tf_op jit(solution)/shard_map/ppermute | solution.py:191
  85.4 1.9 %collective-permute-start.2 = (bf16[128,896]{1,0:T(8,128)(2,1)S(1)}, bf16[128,896]{1,0:T(8,128)(2,1)S(1)}, u32[]{:S(2)}, u32[]{:S(2)}) collective-permute-start(bf16[128,896]{1,0:T(8,128)(2,1)S(1)} %collective-permute-done.1.refs_0_), channel_id=1, source_target_pairs={{0,128},{128,256},{256,384},{384,512},{512,640},{640,768},{768,896... | collective-permute-start | bytes 688136 | tf_op jit(solution)/shard_map/ppermute | solution.py:191
  87.3 5.1 %collective-permute-start.7 = (bf16[128,896]{1,0:T(8,128)(2,1)S(1)}, bf16[128,896]{1,0:T(8,128)(2,1)S(1)}, u32[]{:S(2)}, u32[]{:S(2)}) collective-permute-start(bf16[128,896]{1,0:T(8,128)(2,1)S(1)} %get-tuple-element.43), channel_id=1, source_target_pairs={{0,128},{1,897},{128,256},{129,1},{256,384},{257,129},{384,512},{3... | collective-permute-start | bytes 688136 | tf_op jit(solution)/shard_map/ppermute | solution.py:215
  92.5 1.9 %collective-permute-start.8 = (bf16[128,896]{1,0:T(8,128)(2,1)S(1)}, bf16[128,896]{1,0:T(8,128)(2,1)S(1)}, u32[]{:S(2)}, u32[]{:S(2)}) collective-permute-start(bf16[128,896]{1,0:T(8,128)(2,1)S(1)} %get-tuple-element.44), channel_id=1, source_target_pairs={{0,256},{1,769},{128,384},{129,897},{256,512},{257,1},{384,640},{3... | collective-permute-start | bytes 688136 | tf_op jit(solution)/shard_map/ppermute | solution.py:215
  94.4 3.1 %collective-permute-start.9 = (bf16[128,896]{1,0:T(8,128)(2,1)S(1)}, bf16[128,896]{1,0:T(8,128)(2,1)S(1)}, u32[]{:S(2)}, u32[]{:S(2)}) collective-permute-start(bf16[128,896]{1,0:T(8,128)(2,1)S(1)} %get-tuple-element.45), channel_id=1, source_target_pairs={{0,640},{1,385},{128,768},{129,513},{256,896},{257,641},{384,0},{3... | collective-permute-start | bytes 688136 | tf_op jit(solution)/shard_map/ppermute | solution.py:215
  97.5 6.3 %collective-permute-start.6 = (bf16[128,896]{1,0:T(8,128)(2,1)S(1)}, bf16[128,896]{1,0:T(8,128)(2,1)S(1)}, u32[]{:S(2)}, u32[]{:S(2)}) collective-permute-start(bf16[128,896]{1,0:T(8,128)(2,1)S(1)} %collective-permute-done.5.refs_0_), channel_id=1, source_target_pairs={{0,896},{128,0},{256,128},{384,256},{512,384},{640,512},{768,640},... | collective-permute-start | bytes 688136 | tf_op jit(solution)/shard_map/ppermute | solution.py:194
  103.8 1.9 %collective-permute-start.3 = (bf16[128,896]{1,0:T(8,128)(2,1)S(1)}, bf16[128,896]{1,0:T(8,128)(2,1)S(1)}, u32[]{:S(2)}, u32[]{:S(2)}) collective-permute-start(bf16[128,896]{1,0:T(8,128)(2,1)S(1)} %collective-permute-done.2.refs_0_), channel_id=1, source_target_pairs={{0,128},{128,256},{256,384},{384,512},{512,640},{640,768},{768,896... | collective-permute-start | bytes 688136 | tf_op jit(solution)/shard_map/ppermute | solution.py:191
  105.8 0.8 collective-permute-done.8.refs_1_
  106.6 6.1 %collective-permute-done.9.refs_2_ = bf16[128,896]{1,0:T(8,128)(2,1)S(1)} collective-permute-done((bf16[128,896]{1,0:T(8,128)(2,1)S(1)}, bf16[128,896]{1,0:T(8,128)(2,1)S(1)}, u32[]{:S(2)}, u32[]{:S(2)}) %collective-permute-start.9) | collective-permute-done | bytes 229408 | tf_op jit(solution)/shard_map/ppermute | solution.py:215
  112.7 0.1 stacked.1.mine_ref
  112.8 5.9 %collective-permute-start.11 = (bf16[448,896]{1,0:T(8,128)(2,1)S(1)}, bf16[448,896]{1,0:T(8,128)(2,1)}, u32[]{:S(2)}, u32[]{:S(2)}) collective-permute-start(bf16[448,896]{1,0:T(8,128)(2,1)S(1)} %stacked.1.mine_ref), channel_id=1, source_target_pairs={{0,1},{1,0},{2,3},{3,2},{4,5},{5,4},{6,7},{7,6},{8,9},{9,8},{10,11... | collective-permute-start | bytes 2408456 | tf_op jit(solution)/shard_map/ppermute | solution.py:217
  118.7 0.3 gate_up_step.8
  119.0 0.3 gate_up_step.9
  119.3 0.3 gate_up_step.10
  119.6 0.3 gate_up_step.11
  119.9 0.3 gate_up_step.12
  120.2 0.3 gate_up_step.13
  120.5 0.3 gate_up_step.14
  120.8 0.3 gate_up_step.15
  121.1 0.7 broadcast_in_dim.53
  121.9 3.5 %all-to-all-start.2 = ((bf16[8,128,128]{2,1,0:T(8,128)(2,1)}), bf16[8,128,128]{2,1,0:T(8,128)(2,1)S(1)}, u32[]{:S(2)}, u32[]{:S(2)}) async-start(bf16[8,128,128]{2,1,0:T(8,128)(2,1)} %broadcast_in_dim.53), calls=%async_computation.2 | async-start | bytes 524288 | tf_op jit(solution)/shard_map/all_to_all | solution.py:17
  125.4 3.5 %collective-permute-done.11.others_ref = bf16[448,896]{1,0:T(8,128)(2,1)} collective-permute-done((bf16[448,896]{1,0:T(8,128)(2,1)S(1)}, bf16[448,896]{1,0:T(8,128)(2,1)}, u32[]{:S(2)}, u32[]{:S(2)}) %collective-permute-start.11) | collective-permute-done | bytes 802848 | tf_op jit(solution)/shard_map/ppermute | solution.py:217
  128.9 6.9 %all-to-all-done.2.hid_ref = bf16[8,128,128]{2,1,0:T(8,128)(2,1)S(1)} async-done(((bf16[8,128,128]{2,1,0:T(8,128)(2,1)}), bf16[8,128,128]{2,1,0:T(8,128)(2,1)S(1)}, u32[]{:S(2)}, u32[]{:S(2)}) %all-to-all-start.2) | async-done | bytes 262176 | tf_op jit(solution)/shard_map/all_to_all | solution.py:17
  135.8 1.8 down_product.1
  137.6 0.7 reshape.47
  138.3 5.3 %all-to-all-start.3 = ((bf16[32,4,896]{2,1,0:T(4,128)(2,1)}), bf16[32,4,896]{2,1,0:T(4,128)(2,1)S(1)}, u32[]{:S(2)}, u32[]{:S(2)}) async-start(bf16[32,4,896]{2,1,0:T(4,128)(2,1)} %reshape.47), calls=%async_computation.3 | async-start | bytes 458752 | tf_op jit(solution)/shard_map/all_to_all | solution.py:17
  143.7 21.3 %all-to-all-done.3 = bf16[32,4,896]{2,1,0:T(4,128)(2,1)S(1)} async-done(((bf16[32,4,896]{2,1,0:T(4,128)(2,1)}), bf16[32,4,896]{2,1,0:T(4,128)(2,1)S(1)}, u32[]{:S(2)}, u32[]{:S(2)}) %all-to-all-start.3) | async-done | bytes 229408 | tf_op jit(solution)/shard_map/all_to_all | solution.py:17
  165.0 0.3 fusion
  165.3 13.7 %all_to_all.26 = bf16[16,4,896]{2,1,0:T(4,128)(2,1)S(1)} all-to-all(bf16[16,4,896]{2,1,0:T(4,128)(2,1)S(1)} %reshape.48), channel_id=1, replica_groups=mesh['y'=8,'xh'=2,'z'=16,'core'=2,'dp'=2] {'y','xh'}, dimensions={0} | all-to-all | bytes 229376 | tf_op jit(solution)/shard_map/all_to_all | solution.py:17
  179.0 0.1 bitcast_reduce_fusion
  179.2 0.6 copy-done.5
  (32 shorter events, 0.3 us)
Async XLA Ops:
  0.0 0.8 copy-start.2
  1.5 19.8 %all-to-all-start = ((bf16[16,4,896]{2,1,0:T(4,128)(2,1)}), bf16[16,4,896]{2,1,0:T(4,128)(2,1)S(1)}, u32[]{:S(2)}, u32[]{:S(2)}) async-start(bf16[16,4,896]{2,1,0:T(4,128)(2,1)} %in_columns.1), calls=%async_computation | async-start | bytes 229376 | tf_op jit(solution)/shard_map/all_to_all | solution.py:17
  61.9 56.7 %copy-start.1 = (bf16[1,7168,128]{2,1,0:T(8,128)(2,1)S(1)}, bf16[1,7168,128]{2,1,0:T(8,128)(2,1)}, u32[]{:S(2)}) copy-start(bf16[1,7168,128]{2,1,0:T(8,128)(2,1)} %param.10) | copy-start | bytes 5505028
  62.0 56.7 %copy-start = (bf16[1,7168,128]{2,1,0:T(8,128)(2,1)S(1)}, bf16[1,7168,128]{2,1,0:T(8,128)(2,1)}, u32[]{:S(2)}) copy-start(bf16[1,7168,128]{2,1,0:T(8,128)(2,1)} %param.9) | copy-start | bytes 5505028
  62.0 10.0 %collective-permute-start = (bf16[128,896]{1,0:T(8,128)(2,1)S(1)}, bf16[128,896]{1,0:T(8,128)(2,1)S(1)}, u32[]{:S(2)}, u32[]{:S(2)}) collective-permute-start(bf16[128,896]{1,0:T(8,128)(2,1)S(1)} %reshape.46.refs_0_), channel_id=1, source_target_pairs={{0,128},{128,256},{256,384},{384,512},{512,640},{640,768},{768,896... | collective-permute-start | bytes 688136 | tf_op jit(solution)/shard_map/ppermute | solution.py:191
  64.6 13.5 %collective-permute-start.4 = (bf16[128,896]{1,0:T(8,128)(2,1)S(1)}, bf16[128,896]{1,0:T(8,128)(2,1)S(1)}, u32[]{:S(2)}, u32[]{:S(2)}) collective-permute-start(bf16[128,896]{1,0:T(8,128)(2,1)S(1)} %reshape.46.refs_0_), channel_id=1, source_target_pairs={{0,896},{128,0},{256,128},{384,256},{512,384},{640,512},{768,640},... | collective-permute-start | bytes 688136 | tf_op jit(solution)/shard_map/ppermute | solution.py:194
  72.1 13.3 %collective-permute-start.1 = (bf16[128,896]{1,0:T(8,128)(2,1)S(1)}, bf16[128,896]{1,0:T(8,128)(2,1)S(1)}, u32[]{:S(2)}, u32[]{:S(2)}) collective-permute-start(bf16[128,896]{1,0:T(8,128)(2,1)S(1)} %collective-permute-done.refs_0_), channel_id=1, source_target_pairs={{0,128},{128,256},{256,384},{384,512},{512,640},{640,768},{768,896... | collective-permute-start | bytes 688136 | tf_op jit(solution)/shard_map/ppermute | solution.py:191
  75.4 19.0 %collective-permute-start.10 = (bf16[64,896]{1,0:T(8,128)(2,1)S(1)}, bf16[64,896]{1,0:T(8,128)(2,1)S(1)}, u32[]{:S(2)}, u32[]{:S(2)}) collective-permute-start(bf16[64,896]{1,0:T(8,128)(2,1)S(1)} %get-tuple-element.46), channel_id=1, source_target_pairs={{0,512},{1,513},{128,640},{129,641},{256,768},{257,769},{384,896},... | collective-permute-start | bytes 344072 | tf_op jit(solution)/shard_map/ppermute | solution.py:215
  78.2 19.3 %collective-permute-start.5 = (bf16[128,896]{1,0:T(8,128)(2,1)S(1)}, bf16[128,896]{1,0:T(8,128)(2,1)S(1)}, u32[]{:S(2)}, u32[]{:S(2)}) collective-permute-start(bf16[128,896]{1,0:T(8,128)(2,1)S(1)} %collective-permute-done.4.refs_0_), channel_id=1, source_target_pairs={{0,896},{128,0},{256,128},{384,256},{512,384},{640,512},{768,640},... | collective-permute-start | bytes 688136 | tf_op jit(solution)/shard_map/ppermute | solution.py:194
  85.4 18.4 %collective-permute-start.2 = (bf16[128,896]{1,0:T(8,128)(2,1)S(1)}, bf16[128,896]{1,0:T(8,128)(2,1)S(1)}, u32[]{:S(2)}, u32[]{:S(2)}) collective-permute-start(bf16[128,896]{1,0:T(8,128)(2,1)S(1)} %collective-permute-done.1.refs_0_), channel_id=1, source_target_pairs={{0,128},{128,256},{256,384},{384,512},{512,640},{640,768},{768,896... | collective-permute-start | bytes 688136 | tf_op jit(solution)/shard_map/ppermute | solution.py:191
  87.3 18.4 %collective-permute-start.7 = (bf16[128,896]{1,0:T(8,128)(2,1)S(1)}, bf16[128,896]{1,0:T(8,128)(2,1)S(1)}, u32[]{:S(2)}, u32[]{:S(2)}) collective-permute-start(bf16[128,896]{1,0:T(8,128)(2,1)S(1)} %get-tuple-element.43), channel_id=1, source_target_pairs={{0,128},{1,897},{128,256},{129,1},{256,384},{257,129},{384,512},{3... | collective-permute-start | bytes 688136 | tf_op jit(solution)/shard_map/ppermute | solution.py:215
  92.5 14.1 %collective-permute-start.8 = (bf16[128,896]{1,0:T(8,128)(2,1)S(1)}, bf16[128,896]{1,0:T(8,128)(2,1)S(1)}, u32[]{:S(2)}, u32[]{:S(2)}) collective-permute-start(bf16[128,896]{1,0:T(8,128)(2,1)S(1)} %get-tuple-element.44), channel_id=1, source_target_pairs={{0,256},{1,769},{128,384},{129,897},{256,512},{257,1},{384,640},{3... | collective-permute-start | bytes 688136 | tf_op jit(solution)/shard_map/ppermute | solution.py:215
  94.4 18.3 %collective-permute-start.9 = (bf16[128,896]{1,0:T(8,128)(2,1)S(1)}, bf16[128,896]{1,0:T(8,128)(2,1)S(1)}, u32[]{:S(2)}, u32[]{:S(2)}) collective-permute-start(bf16[128,896]{1,0:T(8,128)(2,1)S(1)} %get-tuple-element.45), channel_id=1, source_target_pairs={{0,640},{1,385},{128,768},{129,513},{256,896},{257,641},{384,0},{3... | collective-permute-start | bytes 688136 | tf_op jit(solution)/shard_map/ppermute | solution.py:215
  97.5 23.0 %collective-permute-start.6 = (bf16[128,896]{1,0:T(8,128)(2,1)S(1)}, bf16[128,896]{1,0:T(8,128)(2,1)S(1)}, u32[]{:S(2)}, u32[]{:S(2)}) collective-permute-start(bf16[128,896]{1,0:T(8,128)(2,1)S(1)} %collective-permute-done.5.refs_0_), channel_id=1, source_target_pairs={{0,896},{128,0},{256,128},{384,256},{512,384},{640,512},{768,640},... | collective-permute-start | bytes 688136 | tf_op jit(solution)/shard_map/ppermute | solution.py:194
  103.8 16.9 %collective-permute-start.3 = (bf16[128,896]{1,0:T(8,128)(2,1)S(1)}, bf16[128,896]{1,0:T(8,128)(2,1)S(1)}, u32[]{:S(2)}, u32[]{:S(2)}) collective-permute-start(bf16[128,896]{1,0:T(8,128)(2,1)S(1)} %collective-permute-done.2.refs_0_), channel_id=1, source_target_pairs={{0,128},{128,256},{256,384},{384,512},{512,640},{640,768},{768,896... | collective-permute-start | bytes 688136 | tf_op jit(solution)/shard_map/ppermute | solution.py:191
  112.8 16.2 %collective-permute-start.11 = (bf16[448,896]{1,0:T(8,128)(2,1)S(1)}, bf16[448,896]{1,0:T(8,128)(2,1)}, u32[]{:S(2)}, u32[]{:S(2)}) collective-permute-start(bf16[448,896]{1,0:T(8,128)(2,1)S(1)} %stacked.1.mine_ref), channel_id=1, source_target_pairs={{0,1},{1,0},{2,3},{3,2},{4,5},{5,4},{6,7},{7,6},{8,9},{9,8},{10,11... | collective-permute-start | bytes 2408456 | tf_op jit(solution)/shard_map/ppermute | solution.py:217
  121.8 21.7 %copy-start.3 = (s32[1,64,8]{1,2,0:T(8,128)S(1)}, s32[1,64,8]{1,2,0:T(8,128)}, u32[]{:S(2)}) copy-start(s32[1,64,8]{1,2,0:T(8,128)} %param.8) | copy-start | bytes 6148
  121.9 21.8 %copy-start.4 = (s32[1,64,8]{1,2,0:T(8,128)S(1)}, s32[1,64,8]{1,2,0:T(8,128)}, u32[]{:S(2)}) copy-start(s32[1,64,8]{1,2,0:T(8,128)} %param.7) | copy-start | bytes 6148
  121.9 14.0 %all-to-all-start.2 = ((bf16[8,128,128]{2,1,0:T(8,128)(2,1)}), bf16[8,128,128]{2,1,0:T(8,128)(2,1)S(1)}, u32[]{:S(2)}, u32[]{:S(2)}) async-start(bf16[8,128,128]{2,1,0:T(8,128)(2,1)} %broadcast_in_dim.53), calls=%async_computation.2 | async-start | bytes 524288 | tf_op jit(solution)/shard_map/all_to_all | solution.py:17
  138.3 26.7 %all-to-all-start.3 = ((bf16[32,4,896]{2,1,0:T(4,128)(2,1)}), bf16[32,4,896]{2,1,0:T(4,128)(2,1)S(1)}, u32[]{:S(2)}, u32[]{:S(2)}) async-start(bf16[32,4,896]{2,1,0:T(4,128)(2,1)} %reshape.47), calls=%async_computation.3 | async-start | bytes 458752 | tf_op jit(solution)/shard_map/all_to_all | solution.py:17
  179.2 0.6 copy-start.5
where the time goes:
time: 181 us; the launch traced here: 180 us
  starting transfers between devices  60.8 us (34%)
  blocking collectives  54 us (30%)
  waiting for transfers between devices  53.6 us (30%)
  Pallas kernels  6.14 us (3%)
  local copies, waits for them, and re-layouts  3.27 us (2%)
    all_to_all x2, blocking collectives, exchange(): return lax.all_to_all(parts, axes, 0, 0, tiled=True)  54 us
    all_to_all x3, waiting for transfers between devices, exchange(): return lax.all_to_all(parts, axes, 0, 0, tiled=True)  38.3 us
    all_to_all x3, starting transfers between devices, exchange(): return lax.all_to_all(parts, axes, 0, 0, tiled=True)  17.6 us
    ppermute x3, starting transfers between devices, around(): b = lax.ppermute(b, axis, down)  16.1 us
    ppermute x4, starting transfers between devices, per_device(): blocks[k - 1] = lax.ppermute(blocks[k - 1], ('y', 'dp'), pairs)  12.9 us
    ppermute x4, starting transfers between devices, around(): a = lax.ppermute(a, axis, up)  8.33 us
    ppermute x4, waiting for transfers between devices, per_device(): blocks[k - 1] = lax.ppermute(blocks[k - 1], ('y', 'dp'), pairs)  6.92 us
    ppermute x1, starting transfers between devices, per_device(): others = lax.ppermute(mine, 'dp', [(0, 1), (1, 0)])  5.91 us
  transfers between devices with their start and end apart: 15, of which 8 were waited for; matrix products, arithmetic and copies ran while one was open for 1% of the time, Pallas kernels for 2%

commit v1 on v0

--- a/solution.py
+++ b/solution.py
@@ -92,21 +92,29 @@
 
 def stacked(parts):
     counts = [p.shape[0] for p in parts]
+    total, cols = sum(counts), parts[0].shape[1]
 
     def kernel(*refs):
-        at = 0
-        for ref, count in zip(refs, counts):
-            refs[-1][at : at + count, :] = ref[...]
+        out_ref, sems = refs[-2:]
+        copies, at = [], 0
+        for k, count in enumerate(counts):
+            place = out_ref.at[pl.ds(at, count), :]
+            copies.append(pltpu.make_async_copy(refs[k], place, sems.at[k]))
             at += count
-
-    return pl.pallas_call(
-        kernel,
-        out_shape=pltpu.VMEM((sum(counts), parts[0].shape[1]), parts[0].dtype),
-        in_specs=[vmem()] * len(parts),
+        for copy in copies:
+            copy.start()
+        for copy in copies:
+            copy.wait()
+
+    return pl.pallas_call(
+        kernel,
+        out_shape=pltpu.VMEM((total, cols), parts[0].dtype),
+        in_specs=[anywhere()] * len(parts),
         out_specs=vmem(),
+        scratch_shapes=[pltpu.SemaphoreType.DMA((len(parts),))],
         name="stacked",
         compiler_params=SMALL,
-    )(*parts)
+    )(*(pltpu.with_memory_space_constraint(p, pltpu.HBM) for p in parts))
 
 
 def down_product(hiddens, own, mine, others):

time: 181 us -> 183 us (1.011)
  transfers between devices with their start and end apart: 15 -> 15, of which waited for: 8 -> 8; matrix products, arithmetic and copies ran while one was open for 1% -> 1% of each run, Pallas kernels for 2% -> 3%
where the time goes in v1:
time: 183 us; the launch traced here: 182 us
  starting transfers between devices  60.8 us (33%)
  blocking collectives  54 us (30%)
  waiting for transfers between devices  53.6 us (29%)
  Pallas kernels  7.34 us (4%)
  local copies, waits for them, and re-layouts  3.96 us (2%)
    all_to_all x2, blocking collectives, exchange(): return lax.all_to_all(parts, axes, 0, 0, tiled=True)  54 us
    all_to_all x3, waiting for transfers between devices, exchange(): return lax.all_to_all(parts, axes, 0, 0, tiled=True)  38.3 us
    all_to_all x3, starting transfers between devices, exchange(): return lax.all_to_all(parts, axes, 0, 0, tiled=True)  17.6 us
    ppermute x3, starting transfers between devices, around(): b = lax.ppermute(b, axis, down)  16.1 us
    ppermute x4, starting transfers between devices, per_device(): blocks[k - 1] = lax.ppermute(blocks[k - 1], ('y', 'dp'), pairs)  12.9 us
    ppermute x4, starting transfers between devices, around(): a = lax.ppermute(a, axis, up)  8.33 us
    ppermute x4, waiting for transfers between devices, per_device(): blocks[k - 1] = lax.ppermute(blocks[k - 1], ('y', 'dp'), pairs)  6.91 us
    ppermute x1, starting transfers between devices, per_device(): others = lax.ppermute(mine, 'dp', [(0, 1), (1, 0)])  5.91 us
  transfers between devices with their start and end apart: 15, of which 8 were waited for; matrix products, arithmetic and copies ran while one was open for 1% of the time, Pallas kernels for 3%

profile of v1, /device:TPU:2, one launch (start us, length us, event | category | flops | bytes accessed | tf_op | source)
XLA Modules:
  0.0 181.8 jit_solution(698038689793895266)
XLA Ops:
  0.0 0.8 copy-done.2
  0.8 0.6 in_columns.1
  1.5 8.8 %all-to-all-start = ((bf16[16,4,896]{2,1,0:T(4,128)(2,1)}), bf16[16,4,896]{2,1,0:T(4,128)(2,1)S(1)}, u32[]{:S(2)}, u32[]{:S(2)}) async-start(bf16[16,4,896]{2,1,0:T(4,128)(2,1)} %in_columns.1), calls=%async_computation | async-start | bytes 229376 | tf_op jit(solution)/shard_map/all_to_all | solution.py:17
  10.2 0.7 fusion.2
  11.0 0.2 fusion.14
  11.2 10.1 %all-to-all-done = bf16[16,4,896]{2,1,0:T(4,128)(2,1)S(1)} async-done(((bf16[16,4,896]{2,1,0:T(4,128)(2,1)}), bf16[16,4,896]{2,1,0:T(4,128)(2,1)S(1)}, u32[]{:S(2)}, u32[]{:S(2)}) %all-to-all-start) | async-done | bytes 114720 | tf_op jit(solution)/shard_map/all_to_all | solution.py:17
  21.3 0.2 convolution_convert_fusion
  21.5 0.1 copy.15
  21.6 40.4 %all_to_all.25 = bf16[32,4,896]{2,1,0:T(4,128)(2,1)S(1)} all-to-all(bf16[32,4,896]{2,1,0:T(4,128)(2,1)S(1)} %copy.15), channel_id=1, replica_groups=mesh['y'=8,'xh'=2,'z'=16,'core'=2,'dp'=2] {'z','core'}, dimensions={0} | all-to-all | bytes 458752 | tf_op jit(solution)/shard_map/all_to_all | solution.py:17
  62.0 2.6 %collective-permute-start = (bf16[128,896]{1,0:T(8,128)(2,1)S(1)}, bf16[128,896]{1,0:T(8,128)(2,1)S(1)}, u32[]{:S(2)}, u32[]{:S(2)}) collective-permute-start(bf16[128,896]{1,0:T(8,128)(2,1)S(1)} %reshape.46.refs_0_), channel_id=1, source_target_pairs={{0,128},{128,256},{256,384},{384,512},{512,640},{640,768},{768,896... | collective-permute-start | bytes 688136 | tf_op jit(solution)/shard_map/ppermute | solution.py:199
  64.6 4.7 %collective-permute-start.4 = (bf16[128,896]{1,0:T(8,128)(2,1)S(1)}, bf16[128,896]{1,0:T(8,128)(2,1)S(1)}, u32[]{:S(2)}, u32[]{:S(2)}) collective-permute-start(bf16[128,896]{1,0:T(8,128)(2,1)S(1)} %reshape.46.refs_0_), channel_id=1, source_target_pairs={{0,896},{128,0},{256,128},{384,256},{512,384},{640,512},{768,640},... | collective-permute-start | bytes 688136 | tf_op jit(solution)/shard_map/ppermute | solution.py:202
  69.3 2.7 %collective-permute-done.refs_0_ = bf16[128,896]{1,0:T(8,128)(2,1)S(1)} collective-permute-done((bf16[128,896]{1,0:T(8,128)(2,1)S(1)}, bf16[128,896]{1,0:T(8,128)(2,1)S(1)}, u32[]{:S(2)}, u32[]{:S(2)}) %collective-permute-start) | collective-permute-done | bytes 229408 | tf_op jit(solution)/shard_map/ppermute | solution.py:199
  72.1 1.9 %collective-permute-start.1 = (bf16[128,896]{1,0:T(8,128)(2,1)S(1)}, bf16[128,896]{1,0:T(8,128)(2,1)S(1)}, u32[]{:S(2)}, u32[]{:S(2)}) collective-permute-start(bf16[128,896]{1,0:T(8,128)(2,1)S(1)} %collective-permute-done.refs_0_), channel_id=1, source_target_pairs={{0,128},{128,256},{256,384},{384,512},{512,640},{640,768},{768,896... | collective-permute-start | bytes 688136 | tf_op jit(solution)/shard_map/ppermute | solution.py:199
  74.0 1.4 cut_blocks.1
  75.4 2.8 %collective-permute-start.10 = (bf16[64,896]{1,0:T(8,128)(2,1)S(1)}, bf16[64,896]{1,0:T(8,128)(2,1)S(1)}, u32[]{:S(2)}, u32[]{:S(2)}) collective-permute-start(bf16[64,896]{1,0:T(8,128)(2,1)S(1)} %get-tuple-element.46), channel_id=1, source_target_pairs={{0,512},{1,513},{128,640},{129,641},{256,768},{257,769},{384,896},... | collective-permute-start | bytes 344072 | tf_op jit(solution)/shard_map/ppermute | solution.py:223
  78.2 5.0 %collective-permute-start.5 = (bf16[128,896]{1,0:T(8,128)(2,1)S(1)}, bf16[128,896]{1,0:T(8,128)(2,1)S(1)}, u32[]{:S(2)}, u32[]{:S(2)}) collective-permute-start(bf16[128,896]{1,0:T(8,128)(2,1)S(1)} %collective-permute-done.4.refs_0_), channel_id=1, source_target_pairs={{0,896},{128,0},{256,128},{384,256},{512,384},{640,512},{768,640},... | collective-permute-start | bytes 688136 | tf_op jit(solution)/shard_map/ppermute | solution.py:202
  83.2 2.2 %collective-permute-done.1.refs_0_ = bf16[128,896]{1,0:T(8,128)(2,1)S(1)} collective-permute-done((bf16[128,896]{1,0:T(8,128)(2,1)S(1)}, bf16[128,896]{1,0:T(8,128)(2,1)S(1)}, u32[]{:S(2)}, u32[]{:S(2)}) %collective-permute-start.1) | collective-permute-done | bytes 229408 | tf_op jit(solution)/shard_map/ppermute | solution.py:199
  85.4 1.9 %collective-permute-start.2 = (bf16[128,896]{1,0:T(8,128)(2,1)S(1)}, bf16[128,896]{1,0:T(8,128)(2,1)S(1)}, u32[]{:S(2)}, u32[]{:S(2)}) collective-permute-start(bf16[128,896]{1,0:T(8,128)(2,1)S(1)} %collective-permute-done.1.refs_0_), channel_id=1, source_target_pairs={{0,128},{128,256},{256,384},{384,512},{512,640},{640,768},{768,896... | collective-permute-start | bytes 688136 | tf_op jit(solution)/shard_map/ppermute | solution.py:199
  87.3 5.1 %collective-permute-start.7 = (bf16[128,896]{1,0:T(8,128)(2,1)S(1)}, bf16[128,896]{1,0:T(8,128)(2,1)S(1)}, u32[]{:S(2)}, u32[]{:S(2)}) collective-permute-start(bf16[128,896]{1,0:T(8,128)(2,1)S(1)} %get-tuple-element.43), channel_id=1, source_target_pairs={{0,128},{1,897},{128,256},{129,1},{256,384},{257,129},{384,512},{3... | collective-permute-start | bytes 688136 | tf_op jit(solution)/shard_map/ppermute | solution.py:223
  92.5 1.9 %collective-permute-start.8 = (bf16[128,896]{1,0:T(8,128)(2,1)S(1)}, bf16[128,896]{1,0:T(8,128)(2,1)S(1)}, u32[]{:S(2)}, u32[]{:S(2)}) collective-permute-start(bf16[128,896]{1,0:T(8,128)(2,1)S(1)} %get-tuple-element.44), channel_id=1, source_target_pairs={{0,256},{1,769},{128,384},{129,897},{256,512},{257,1},{384,640},{3... | collective-permute-start | bytes 688136 | tf_op jit(solution)/shard_map/ppermute | solution.py:223
  94.4 3.1 %collective-permute-start.9 = (bf16[128,896]{1,0:T(8,128)(2,1)S(1)}, bf16[128,896]{1,0:T(8,128)(2,1)S(1)}, u32[]{:S(2)}, u32[]{:S(2)}) collective-permute-start(bf16[128,896]{1,0:T(8,128)(2,1)S(1)} %get-tuple-element.45), channel_id=1, source_target_pairs={{0,640},{1,385},{128,768},{129,513},{256,896},{257,641},{384,0},{3... | collective-permute-start | bytes 688136 | tf_op jit(solution)/shard_map/ppermute | solution.py:223
  97.5 6.3 %collective-permute-start.6 = (bf16[128,896]{1,0:T(8,128)(2,1)S(1)}, bf16[128,896]{1,0:T(8,128)(2,1)S(1)}, u32[]{:S(2)}, u32[]{:S(2)}) collective-permute-start(bf16[128,896]{1,0:T(8,128)(2,1)S(1)} %collective-permute-done.5.refs_0_), channel_id=1, source_target_pairs={{0,896},{128,0},{256,128},{384,256},{512,384},{640,512},{768,640},... | collective-permute-start | bytes 688136 | tf_op jit(solution)/shard_map/ppermute | solution.py:202
  103.8 1.9 %collective-permute-start.3 = (bf16[128,896]{1,0:T(8,128)(2,1)S(1)}, bf16[128,896]{1,0:T(8,128)(2,1)S(1)}, u32[]{:S(2)}, u32[]{:S(2)}) collective-permute-start(bf16[128,896]{1,0:T(8,128)(2,1)S(1)} %collective-permute-done.2.refs_0_), channel_id=1, source_target_pairs={{0,128},{128,256},{256,384},{384,512},{512,640},{640,768},{768,896... | collective-permute-start | bytes 688136 | tf_op jit(solution)/shard_map/ppermute | solution.py:199
  105.8 0.8 collective-permute-done.8.refs_1_
  106.6 6.1 %collective-permute-done.9.refs_2_ = bf16[128,896]{1,0:T(8,128)(2,1)S(1)} collective-permute-done((bf16[128,896]{1,0:T(8,128)(2,1)S(1)}, bf16[128,896]{1,0:T(8,128)(2,1)S(1)}, u32[]{:S(2)}, u32[]{:S(2)}) %collective-permute-start.9) | collective-permute-done | bytes 229408 | tf_op jit(solution)/shard_map/ppermute | solution.py:223
  112.7 0.7 copy-done.5
  113.4 1.3 stacked.1.mine_ref
  114.7 5.9 %collective-permute-start.11 = (bf16[448,896]{1,0:T(8,128)(2,1)S(1)}, bf16[448,896]{1,0:T(8,128)(2,1)}, u32[]{:S(2)}, u32[]{:S(2)}) collective-permute-start(bf16[448,896]{1,0:T(8,128)(2,1)S(1)} %stacked.1.mine_ref), channel_id=1, source_target_pairs={{0,1},{1,0},{2,3},{3,2},{4,5},{5,4},{6,7},{7,6},{8,9},{9,8},{10,11... | collective-permute-start | bytes 2408456 | tf_op jit(solution)/shard_map/ppermute | solution.py:225
  120.6 0.3 gate_up_step.8
  120.9 0.3 gate_up_step.9
  121.2 0.3 gate_up_step.10
  121.5 0.3 gate_up_step.11
  121.8 0.3 gate_up_step.12
  122.1 0.3 gate_up_step.13
  122.4 0.3 gate_up_step.14
  122.7 0.3 gate_up_step.15
  123.0 0.7 broadcast_in_dim.53
  123.8 3.5 %all-to-all-start.2 = ((bf16[8,128,128]{2,1,0:T(8,128)(2,1)}), bf16[8,128,128]{2,1,0:T(8,128)(2,1)S(1)}, u32[]{:S(2)}, u32[]{:S(2)}) async-start(bf16[8,128,128]{2,1,0:T(8,128)(2,1)} %broadcast_in_dim.53), calls=%async_computation.2 | async-start | bytes 524288 | tf_op jit(solution)/shard_map/all_to_all | solution.py:17
  127.3 3.5 %collective-permute-done.11.others_ref = bf16[448,896]{1,0:T(8,128)(2,1)} collective-permute-done((bf16[448,896]{1,0:T(8,128)(2,1)S(1)}, bf16[448,896]{1,0:T(8,128)(2,1)}, u32[]{:S(2)}, u32[]{:S(2)}) %collective-permute-start.11) | collective-permute-done | bytes 802848 | tf_op jit(solution)/shard_map/ppermute | solution.py:225
  130.8 6.9 %all-to-all-done.2.hid_ref = bf16[8,128,128]{2,1,0:T(8,128)(2,1)S(1)} async-done(((bf16[8,128,128]{2,1,0:T(8,128)(2,1)}), bf16[8,128,128]{2,1,0:T(8,128)(2,1)S(1)}, u32[]{:S(2)}, u32[]{:S(2)}) %all-to-all-start.2) | async-done | bytes 262176 | tf_op jit(solution)/shard_map/all_to_all | solution.py:17
  137.7 1.8 down_product.1
  139.5 0.7 reshape.47
  140.2 5.3 %all-to-all-start.3 = ((bf16[32,4,896]{2,1,0:T(4,128)(2,1)}), bf16[32,4,896]{2,1,0:T(4,128)(2,1)S(1)}, u32[]{:S(2)}, u32[]{:S(2)}) async-start(bf16[32,4,896]{2,1,0:T(4,128)(2,1)} %reshape.47), calls=%async_computation.3 | async-start | bytes 458752 | tf_op jit(solution)/shard_map/all_to_all | solution.py:17
  145.6 21.3 %all-to-all-done.3 = bf16[32,4,896]{2,1,0:T(4,128)(2,1)S(1)} async-done(((bf16[32,4,896]{2,1,0:T(4,128)(2,1)}), bf16[32,4,896]{2,1,0:T(4,128)(2,1)S(1)}, u32[]{:S(2)}, u32[]{:S(2)}) %all-to-all-start.3) | async-done | bytes 229408 | tf_op jit(solution)/shard_map/all_to_all | solution.py:17
  166.9 0.3 fusion
  167.2 13.7 %all_to_all.26 = bf16[16,4,896]{2,1,0:T(4,128)(2,1)S(1)} all-to-all(bf16[16,4,896]{2,1,0:T(4,128)(2,1)S(1)} %reshape.48), channel_id=1, replica_groups=mesh['y'=8,'xh'=2,'z'=16,'core'=2,'dp'=2] {'y','xh'}, dimensions={0} | all-to-all | bytes 229376 | tf_op jit(solution)/shard_map/all_to_all | solution.py:17
  180.9 0.1 bitcast_reduce_fusion
  181.1 0.6 copy-done.9
  (40 shorter events, 0.4 us)
Async XLA Ops:
  0.0 0.8 copy-start.2
  1.5 19.8 %all-to-all-start = ((bf16[16,4,896]{2,1,0:T(4,128)(2,1)}), bf16[16,4,896]{2,1,0:T(4,128)(2,1)S(1)}, u32[]{:S(2)}, u32[]{:S(2)}) async-start(bf16[16,4,896]{2,1,0:T(4,128)(2,1)} %in_columns.1), calls=%async_computation | async-start | bytes 229376 | tf_op jit(solution)/shard_map/all_to_all | solution.py:17
  61.9 58.7 %copy-start.1 = (bf16[1,7168,128]{2,1,0:T(8,128)(2,1)S(1)}, bf16[1,7168,128]{2,1,0:T(8,128)(2,1)}, u32[]{:S(2)}) copy-start(bf16[1,7168,128]{2,1,0:T(8,128)(2,1)} %param.10) | copy-start | bytes 5505028
  62.0 58.6 %copy-start = (bf16[1,7168,128]{2,1,0:T(8,128)(2,1)S(1)}, bf16[1,7168,128]{2,1,0:T(8,128)(2,1)}, u32[]{:S(2)}) copy-start(bf16[1,7168,128]{2,1,0:T(8,128)(2,1)} %param.9) | copy-start | bytes 5505028
  62.0 10.0 %collective-permute-start = (bf16[128,896]{1,0:T(8,128)(2,1)S(1)}, bf16[128,896]{1,0:T(8,128)(2,1)S(1)}, u32[]{:S(2)}, u32[]{:S(2)}) collective-permute-start(bf16[128,896]{1,0:T(8,128)(2,1)S(1)} %reshape.46.refs_0_), channel_id=1, source_target_pairs={{0,128},{128,256},{256,384},{384,512},{512,640},{640,768},{768,896... | collective-permute-start | bytes 688136 | tf_op jit(solution)/shard_map/ppermute | solution.py:199
  64.6 13.5 %collective-permute-start.4 = (bf16[128,896]{1,0:T(8,128)(2,1)S(1)}, bf16[128,896]{1,0:T(8,128)(2,1)S(1)}, u32[]{:S(2)}, u32[]{:S(2)}) collective-permute-start(bf16[128,896]{1,0:T(8,128)(2,1)S(1)} %reshape.46.refs_0_), channel_id=1, source_target_pairs={{0,896},{128,0},{256,128},{384,256},{512,384},{640,512},{768,640},... | collective-permute-start | bytes 688136 | tf_op jit(solution)/shard_map/ppermute | solution.py:202
  72.1 13.3 %collective-permute-start.1 = (bf16[128,896]{1,0:T(8,128)(2,1)S(1)}, bf16[128,896]{1,0:T(8,128)(2,1)S(1)}, u32[]{:S(2)}, u32[]{:S(2)}) collective-permute-start(bf16[128,896]{1,0:T(8,128)(2,1)S(1)} %collective-permute-done.refs_0_), channel_id=1, source_target_pairs={{0,128},{128,256},{256,384},{384,512},{512,640},{640,768},{768,896... | collective-permute-start | bytes 688136 | tf_op jit(solution)/shard_map/ppermute | solution.py:199
  75.4 19.0 %collective-permute-start.10 = (bf16[64,896]{1,0:T(8,128)(2,1)S(1)}, bf16[64,896]{1,0:T(8,128)(2,1)S(1)}, u32[]{:S(2)}, u32[]{:S(2)}) collective-permute-start(bf16[64,896]{1,0:T(8,128)(2,1)S(1)} %get-tuple-element.46), channel_id=1, source_target_pairs={{0,512},{1,513},{128,640},{129,641},{256,768},{257,769},{384,896},... | collective-permute-start | bytes 344072 | tf_op jit(solution)/shard_map/ppermute | solution.py:223
  78.2 19.3 %collective-permute-start.5 = (bf16[128,896]{1,0:T(8,128)(2,1)S(1)}, bf16[128,896]{1,0:T(8,128)(2,1)S(1)}, u32[]{:S(2)}, u32[]{:S(2)}) collective-permute-start(bf16[128,896]{1,0:T(8,128)(2,1)S(1)} %collective-permute-done.4.refs_0_), channel_id=1, source_target_pairs={{0,896},{128,0},{256,128},{384,256},{512,384},{640,512},{768,640},... | collective-permute-start | bytes 688136 | tf_op jit(solution)/shard_map/ppermute | solution.py:202
  85.4 18.4 %collective-permute-start.2 = (bf16[128,896]{1,0:T(8,128)(2,1)S(1)}, bf16[128,896]{1,0:T(8,128)(2,1)S(1)}, u32[]{:S(2)}, u32[]{:S(2)}) collective-permute-start(bf16[128,896]{1,0:T(8,128)(2,1)S(1)} %collective-permute-done.1.refs_0_), channel_id=1, source_target_pairs={{0,128},{128,256},{256,384},{384,512},{512,640},{640,768},{768,896... | collective-permute-start | bytes 688136 | tf_op jit(solution)/shard_map/ppermute | solution.py:199
  87.3 18.5 %collective-permute-start.7 = (bf16[128,896]{1,0:T(8,128)(2,1)S(1)}, bf16[128,896]{1,0:T(8,128)(2,1)S(1)}, u32[]{:S(2)}, u32[]{:S(2)}) collective-permute-start(bf16[128,896]{1,0:T(8,128)(2,1)S(1)} %get-tuple-element.43), channel_id=1, source_target_pairs={{0,128},{1,897},{128,256},{129,1},{256,384},{257,129},{384,512},{3... | collective-permute-start | bytes 688136 | tf_op jit(solution)/shard_map/ppermute | solution.py:223
  92.5 14.1 %collective-permute-start.8 = (bf16[128,896]{1,0:T(8,128)(2,1)S(1)}, bf16[128,896]{1,0:T(8,128)(2,1)S(1)}, u32[]{:S(2)}, u32[]{:S(2)}) collective-permute-start(bf16[128,896]{1,0:T(8,128)(2,1)S(1)} %get-tuple-element.44), channel_id=1, source_target_pairs={{0,256},{1,769},{128,384},{129,897},{256,512},{257,1},{384,640},{3... | collective-permute-start | bytes 688136 | tf_op jit(solution)/shard_map/ppermute | solution.py:223
  94.4 18.3 %copy-start.6 = (bf16[64,896]{1,0:T(8,128)(2,1)}, bf16[64,896]{1,0:T(8,128)(2,1)S(1)}, u32[]{:S(2)}) copy-start(bf16[64,896]{1,0:T(8,128)(2,1)S(1)} %collective-permute-done.10.refs_3_) | copy-start | bytes 344068
  94.4 18.3 %collective-permute-start.9 = (bf16[128,896]{1,0:T(8,128)(2,1)S(1)}, bf16[128,896]{1,0:T(8,128)(2,1)S(1)}, u32[]{:S(2)}, u32[]{:S(2)}) collective-permute-start(bf16[128,896]{1,0:T(8,128)(2,1)S(1)} %get-tuple-element.45), channel_id=1, source_target_pairs={{0,640},{1,385},{128,768},{129,513},{256,896},{257,641},{384,0},{3... | collective-permute-start | bytes 688136 | tf_op jit(solution)/shard_map/ppermute | solution.py:223
  97.5 24.9 %collective-permute-start.6 = (bf16[128,896]{1,0:T(8,128)(2,1)S(1)}, bf16[128,896]{1,0:T(8,128)(2,1)S(1)}, u32[]{:S(2)}, u32[]{:S(2)}) collective-permute-start(bf16[128,896]{1,0:T(8,128)(2,1)S(1)} %collective-permute-done.5.refs_0_), channel_id=1, source_target_pairs={{0,896},{128,0},{256,128},{384,256},{512,384},{640,512},{768,640},... | collective-permute-start | bytes 688136 | tf_op jit(solution)/shard_map/ppermute | solution.py:202
  103.8 18.8 %collective-permute-start.3 = (bf16[128,896]{1,0:T(8,128)(2,1)S(1)}, bf16[128,896]{1,0:T(8,128)(2,1)S(1)}, u32[]{:S(2)}, u32[]{:S(2)}) collective-permute-start(bf16[128,896]{1,0:T(8,128)(2,1)S(1)} %collective-permute-done.2.refs_0_), channel_id=1, source_target_pairs={{0,128},{128,256},{256,384},{384,512},{512,640},{640,768},{768,896... | collective-permute-start | bytes 688136 | tf_op jit(solution)/shard_map/ppermute | solution.py:199
  105.8 6.9 %copy-start.3 = (bf16[128,896]{1,0:T(8,128)(2,1)}, bf16[128,896]{1,0:T(8,128)(2,1)S(1)}, u32[]{:S(2)}) copy-start(bf16[128,896]{1,0:T(8,128)(2,1)S(1)} %collective-permute-done.7.refs_0_) | copy-start | bytes 688132
  106.6 6.1 %copy-start.4 = (bf16[128,896]{1,0:T(8,128)(2,1)}, bf16[128,896]{1,0:T(8,128)(2,1)S(1)}, u32[]{:S(2)}) copy-start(bf16[128,896]{1,0:T(8,128)(2,1)S(1)} %collective-permute-done.8.refs_1_) | copy-start | bytes 688132
  112.7 0.7 copy-start.5
  114.7 16.2 %collective-permute-start.11 = (bf16[448,896]{1,0:T(8,128)(2,1)S(1)}, bf16[448,896]{1,0:T(8,128)(2,1)}, u32[]{:S(2)}, u32[]{:S(2)}) collective-permute-start(bf16[448,896]{1,0:T(8,128)(2,1)S(1)} %stacked.1.mine_ref), channel_id=1, source_target_pairs={{0,1},{1,0},{2,3},{3,2},{4,5},{5,4},{6,7},{7,6},{8,9},{9,8},{10,11... | collective-permute-start | bytes 2408456 | tf_op jit(solution)/shard_map/ppermute | solution.py:225
  123.8 21.7 %copy-start.7 = (s32[1,64,8]{1,2,0:T(8,128)S(1)}, s32[1,64,8]{1,2,0:T(8,128)}, u32[]{:S(2)}) copy-start(s32[1,64,8]{1,2,0:T(8,128)} %param.8) | copy-start | bytes 6148
  123.8 21.8 %copy-start.8 = (s32[1,64,8]{1,2,0:T(8,128)S(1)}, s32[1,64,8]{1,2,0:T(8,128)}, u32[]{:S(2)}) copy-start(s32[1,64,8]{1,2,0:T(8,128)} %param.7) | copy-start | bytes 6148
  123.8 13.9 %all-to-all-start.2 = ((bf16[8,128,128]{2,1,0:T(8,128)(2,1)}), bf16[8,128,128]{2,1,0:T(8,128)(2,1)S(1)}, u32[]{:S(2)}, u32[]{:S(2)}) async-start(bf16[8,128,128]{2,1,0:T(8,128)(2,1)} %broadcast_in_dim.53), calls=%async_computation.2 | async-start | bytes 524288 | tf_op jit(solution)/shard_map/all_to_all | solution.py:17
  140.2 26.7 %all-to-all-start.3 = ((bf16[32,4,896]{2,1,0:T(4,128)(2,1)}), bf16[32,4,896]{2,1,0:T(4,128)(2,1)S(1)}, u32[]{:S(2)}, u32[]{:S(2)}) async-start(bf16[32,4,896]{2,1,0:T(4,128)(2,1)} %reshape.47), calls=%async_computation.3 | async-start | bytes 458752 | tf_op jit(solution)/shard_map/all_to_all | solution.py:17
  181.1 0.6 copy-start.9

commit v2 on v1

--- a/solution.py
+++ b/solution.py
@@ -149,7 +149,7 @@
     )(*(in_vmem(x) for x in (hiddens, own, mine, others)))
 
 
-def gate_up_step(sums, shard, gate, up, step, axis):
+def gate_up_step(sums, shard, gate, up, step, axis, last):
     n = lax.axis_size(axis)
     rows, cols = shard.shape
     hid = gate.shape[1]
@@ -160,15 +160,23 @@
         here = lax.axis_index(axis)
         at = pl.multiple_of(lax.rem(here + step + n, n) * cols, cols)
         block = shard_ref[...]
+        got = []
         for i, weight in enumerate((gate_ref, up_ref)):
-            got = jnp.dot(block, weight[pl.ds(at, cols), :], preferred_element_type=jnp.float32)
-            refs[-2 + i][...] = got if first else refs[3 + i][...] + got
-
-    return pl.pallas_call(
-        kernel,
-        out_shape=[pltpu.VMEM((rows, hid), jnp.float32)] * 2,
+            part = jnp.dot(block, weight[pl.ds(at, cols), :], preferred_element_type=jnp.float32)
+            got.append(part if first else refs[3 + i][...] + part)
+        if last:
+            hidden = (jax.nn.silu(got[0]) * got[1]).astype(jnp.bfloat16)
+            for i in range(n):
+                refs[-1][i] = hidden
+        else:
+            refs[-2][...], refs[-1][...] = got
+
+    sum_out = [pltpu.VMEM((rows, hid), jnp.float32)] * 2
+    return pl.pallas_call(
+        kernel,
+        out_shape=jax.ShapeDtypeStruct((n, rows, hid), jnp.bfloat16) if last else sum_out,
         in_specs=[vmem()] * (3 if first else 5),
-        out_specs=[vmem()] * 2,
+        out_specs=vmem() if last else [vmem()] * 2,
         name="gate_up_step",
         compiler_params=SMALL,
     )(*(in_vmem(x) for x in (shard, gate, up, *(sums or ()))))
@@ -209,7 +217,6 @@
     experts = lax.axis_size(EXPERT)
     own, width = tokens.shape[1], tokens.shape[2]
     cols = width // ny
-    hid = w_gate.shape[2]
 
     toks = exchange(in_columns(tokens[0], ny, nh), GROUP)
     own_block, *blocks = cut_blocks(w_down[0])
@@ -236,11 +243,11 @@
     sets = got.shape[0]
     count = sets * CAPG
     sums = None
-    for step, shard in around(got.reshape(count, cols), "y"):
-        sums = gate_up_step(sums, shard, w_gate[0], w_up[0], step, "y")
-    first, second = sums
-    hidden = (jax.nn.silu(first) * second).astype(jnp.bfloat16)
-    hiddens = exchange(jnp.broadcast_to(hidden[None], (ny, count, hid)), "y")
+    shards = around(got.reshape(count, cols), "y")
+    for step, shard in shards:
+        last = shard is shards[-1][1]
+        sums = gate_up_step(sums, shard, w_gate[0], w_up[0], step, "y", last)
+    hiddens = exchange(sums, "y")
     outs = down_product(hiddens, own_block, mine, others)
     back = exchange(outs.reshape(sets, CAPG, cols), EXPERT)
     mixed = jnp.einsum(

time: 183 us -> 186 us (1.016)
  waiting for transfers between devices: 53.6 us -> 55.6 us
    ppermute x3, starting transfers between devices: 16.1 us -> 11.2 us  [around(): b = lax.ppermute(b, axis, down)]
    ppermute x1, waiting for transfers between devices: 3.51 us -> 0.01 us  [per_device(): others = lax.ppermute(mine, 'dp', [(0, 1), (1, 0)])]
    all_to_all x3, waiting for transfers between devices: 38.3 us -> 41.8 us  [exchange(): return lax.all_to_all(parts, axes, 0, 0, tiled=True)]
    ppermute x4, waiting for transfers between devices: 6.91 us -> 8.79 us  [per_device(): blocks[k - 1] = lax.ppermute(blocks[k - 1], ('y', 'dp'), pairs)]
  transfers between devices with their start and end apart: 15 -> 15, of which waited for: 8 -> 9; matrix products, arithmetic and copies ran while one was open for 1% -> 1% of each run, Pallas kernels for 3% -> 3%
where the time goes in v2:
time: 186 us; the launch traced here: 185 us
  starting transfers between devices  62.1 us (33%)
  waiting for transfers between devices  55.6 us (30%)
  blocking collectives  54 us (29%)
  Pallas kernels  8.04 us (4%)
  local copies, waits for them, and re-layouts  3.23 us (2%)
    all_to_all x2, blocking collectives, exchange(): return lax.all_to_all(parts, axes, 0, 0, tiled=True)  54 us
    all_to_all x3, waiting for transfers between devices, exchange(): return lax.all_to_all(parts, axes, 0, 0, tiled=True)  41.8 us
    all_to_all x3, starting transfers between devices, exchange(): return lax.all_to_all(parts, axes, 0, 0, tiled=True)  19 us
    ppermute x4, starting transfers between devices, per_device(): blocks[k - 1] = lax.ppermute(blocks[k - 1], ('y', 'dp'), pairs)  14.6 us
    ppermute x3, starting transfers between devices, around(): b = lax.ppermute(b, axis, down)  11.2 us
    ppermute x4, starting transfers between devices, around(): a = lax.ppermute(a, axis, up)  9.76 us
    ppermute x4, waiting for transfers between devices, per_device(): blocks[k - 1] = lax.ppermute(blocks[k - 1], ('y', 'dp'), pairs)  8.79 us
    ppermute x1, starting transfers between devices, per_device(): others = lax.ppermute(mine, 'dp', [(0, 1), (1, 0)])  7.58 us
  transfers between devices with their start and end apart: 15, of which 9 were waited for; matrix products, arithmetic and copies ran while one was open for 1% of the time, Pallas kernels for 3%

profile of v2, /device:TPU:2, one launch (start us, length us, event | category | flops | bytes accessed | tf_op | source)
XLA Modules:
  0.0 185.0 jit_solution(6651584848476086404)
XLA Ops:
  0.0 0.8 copy-done.2
  0.8 0.6 in_columns.1
  1.5 8.8 %all-to-all-start = ((bf16[16,4,896]{2,1,0:T(4,128)(2,1)}), bf16[16,4,896]{2,1,0:T(4,128)(2,1)S(1)}, u32[]{:S(2)}, u32[]{:S(2)}) async-start(bf16[16,4,896]{2,1,0:T(4,128)(2,1)} %in_columns.1), calls=%async_computation | async-start | bytes 229376 | tf_op jit(solution)/shard_map/all_to_all | solution.py:17
  10.3 0.7 fusion.2
  11.0 0.2 fusion.14
  11.2 10.1 %all-to-all-done = bf16[16,4,896]{2,1,0:T(4,128)(2,1)S(1)} async-done(((bf16[16,4,896]{2,1,0:T(4,128)(2,1)}), bf16[16,4,896]{2,1,0:T(4,128)(2,1)S(1)}, u32[]{:S(2)}, u32[]{:S(2)}) %all-to-all-start) | async-done | bytes 114720 | tf_op jit(solution)/shard_map/all_to_all | solution.py:17
  21.3 0.2 convolution_convert_fusion
  21.5 0.1 copy.15
  21.6 40.4 %all_to_all.25 = bf16[32,4,896]{2,1,0:T(4,128)(2,1)S(1)} all-to-all(bf16[32,4,896]{2,1,0:T(4,128)(2,1)S(1)} %copy.15), channel_id=1, replica_groups=mesh['y'=8,'xh'=2,'z'=16,'core'=2,'dp'=2] {'z','core'}, dimensions={0} | all-to-all | bytes 458752 | tf_op jit(solution)/shard_map/all_to_all | solution.py:17
  62.0 2.6 %collective-permute-start = (bf16[128,896]{1,0:T(8,128)(2,1)S(1)}, bf16[128,896]{1,0:T(8,128)(2,1)S(1)}, u32[]{:S(2)}, u32[]{:S(2)}) collective-permute-start(bf16[128,896]{1,0:T(8,128)(2,1)S(1)} %reshape.45.refs_0_), channel_id=1, source_target_pairs={{0,128},{128,256},{256,384},{384,512},{512,640},{640,768},{768,896... | collective-permute-start | bytes 688136 | tf_op jit(solution)/shard_map/ppermute | solution.py:207
  64.6 4.7 %collective-permute-start.4 = (bf16[128,896]{1,0:T(8,128)(2,1)S(1)}, bf16[128,896]{1,0:T(8,128)(2,1)S(1)}, u32[]{:S(2)}, u32[]{:S(2)}) collective-permute-start(bf16[128,896]{1,0:T(8,128)(2,1)S(1)} %reshape.45.refs_0_), channel_id=1, source_target_pairs={{0,896},{128,0},{256,128},{384,256},{512,384},{640,512},{768,640},... | collective-permute-start | bytes 688136 | tf_op jit(solution)/shard_map/ppermute | solution.py:210
  69.4 1.4 cut_blocks.1
  70.7 1.3 collective-permute-done.refs_0_
  72.1 1.9 %collective-permute-start.1 = (bf16[128,896]{1,0:T(8,128)(2,1)S(1)}, bf16[128,896]{1,0:T(8,128)(2,1)S(1)}, u32[]{:S(2)}, u32[]{:S(2)}) collective-permute-start(bf16[128,896]{1,0:T(8,128)(2,1)S(1)} %collective-permute-done.refs_0_), channel_id=1, source_target_pairs={{0,128},{128,256},{256,384},{384,512},{512,640},{640,768},{768,896... | collective-permute-start | bytes 688136 | tf_op jit(solution)/shard_map/ppermute | solution.py:207
  74.0 2.8 %collective-permute-start.10 = (bf16[64,896]{1,0:T(8,128)(2,1)S(1)}, bf16[64,896]{1,0:T(8,128)(2,1)S(1)}, u32[]{:S(2)}, u32[]{:S(2)}) collective-permute-start(bf16[64,896]{1,0:T(8,128)(2,1)S(1)} %get-tuple-element.42), channel_id=1, source_target_pairs={{0,512},{1,513},{128,640},{129,641},{256,768},{257,769},{384,896},... | collective-permute-start | bytes 344072 | tf_op jit(solution)/shard_map/ppermute | solution.py:230
  76.8 5.0 %collective-permute-start.7 = (bf16[128,896]{1,0:T(8,128)(2,1)S(1)}, bf16[128,896]{1,0:T(8,128)(2,1)S(1)}, u32[]{:S(2)}, u32[]{:S(2)}) collective-permute-start(bf16[128,896]{1,0:T(8,128)(2,1)S(1)} %get-tuple-element.39), channel_id=1, source_target_pairs={{0,128},{1,897},{128,256},{129,1},{256,384},{257,129},{384,512},{3... | collective-permute-start | bytes 688136 | tf_op jit(solution)/shard_map/ppermute | solution.py:230
  81.8 2.9 %collective-permute-start.8 = (bf16[128,896]{1,0:T(8,128)(2,1)S(1)}, bf16[128,896]{1,0:T(8,128)(2,1)S(1)}, u32[]{:S(2)}, u32[]{:S(2)}) collective-permute-start(bf16[128,896]{1,0:T(8,128)(2,1)S(1)} %get-tuple-element.40), channel_id=1, source_target_pairs={{0,256},{1,769},{128,384},{129,897},{256,512},{257,1},{384,640},{3... | collective-permute-start | bytes 688136 | tf_op jit(solution)/shard_map/ppermute | solution.py:230
  84.8 1.1 collective-permute-done.10.refs_3_
  85.9 3.9 %collective-permute-start.9 = (bf16[128,896]{1,0:T(8,128)(2,1)S(1)}, bf16[128,896]{1,0:T(8,128)(2,1)S(1)}, u32[]{:S(2)}, u32[]{:S(2)}) collective-permute-start(bf16[128,896]{1,0:T(8,128)(2,1)S(1)} %get-tuple-element.41), channel_id=1, source_target_pairs={{0,640},{1,385},{128,768},{129,513},{256,896},{257,641},{384,0},{3... | collective-permute-start | bytes 688136 | tf_op jit(solution)/shard_map/ppermute | solution.py:230
  89.8 3.9 %collective-permute-start.5 = (bf16[128,896]{1,0:T(8,128)(2,1)S(1)}, bf16[128,896]{1,0:T(8,128)(2,1)S(1)}, u32[]{:S(2)}, u32[]{:S(2)}) collective-permute-start(bf16[128,896]{1,0:T(8,128)(2,1)S(1)} %collective-permute-done.4.refs_0_), channel_id=1, source_target_pairs={{0,896},{128,0},{256,128},{384,256},{512,384},{640,512},{768,640},... | collective-permute-start | bytes 688136 | tf_op jit(solution)/shard_map/ppermute | solution.py:210
  93.7 1.9 %collective-permute-start.2 = (bf16[128,896]{1,0:T(8,128)(2,1)S(1)}, bf16[128,896]{1,0:T(8,128)(2,1)S(1)}, u32[]{:S(2)}, u32[]{:S(2)}) collective-permute-start(bf16[128,896]{1,0:T(8,128)(2,1)S(1)} %collective-permute-done.1.refs_0_), channel_id=1, source_target_pairs={{0,128},{128,256},{256,384},{384,512},{512,640},{640,768},{768,896... | collective-permute-start | bytes 688136 | tf_op jit(solution)/shard_map/ppermute | solution.py:207
  95.7 4.0 %collective-permute-done.8.refs_1_ = bf16[128,896]{1,0:T(8,128)(2,1)S(1)} collective-permute-done((bf16[128,896]{1,0:T(8,128)(2,1)S(1)}, bf16[128,896]{1,0:T(8,128)(2,1)S(1)}, u32[]{:S(2)}, u32[]{:S(2)}) %collective-permute-start.8) | collective-permute-done | bytes 229408 | tf_op jit(solution)/shard_map/ppermute | solution.py:230
  99.7 3.6 %collective-permute-done.9.refs_2_ = bf16[128,896]{1,0:T(8,128)(2,1)S(1)} collective-permute-done((bf16[128,896]{1,0:T(8,128)(2,1)S(1)}, bf16[128,896]{1,0:T(8,128)(2,1)S(1)}, u32[]{:S(2)}, u32[]{:S(2)}) %collective-permute-start.9) | collective-permute-done | bytes 229408 | tf_op jit(solution)/shard_map/ppermute | solution.py:230
  103.3 0.7 copy-done.5
  104.0 1.3 stacked.1.mine_ref
  105.3 7.6 %collective-permute-start.11 = (bf16[448,896]{1,0:T(8,128)(2,1)S(1)}, bf16[448,896]{1,0:T(8,128)(2,1)}, u32[]{:S(2)}, u32[]{:S(2)}) collective-permute-start(bf16[448,896]{1,0:T(8,128)(2,1)S(1)} %stacked.1.mine_ref), channel_id=1, source_target_pairs={{0,1},{1,0},{2,3},{3,2},{4,5},{5,4},{6,7},{7,6},{8,9},{9,8},{10,11... | collective-permute-start | bytes 2408456 | tf_op jit(solution)/shard_map/ppermute | solution.py:232
  112.9 2.5 %collective-permute-start.6 = (bf16[128,896]{1,0:T(8,128)(2,1)S(1)}, bf16[128,896]{1,0:T(8,128)(2,1)S(1)}, u32[]{:S(2)}, u32[]{:S(2)}) collective-permute-start(bf16[128,896]{1,0:T(8,128)(2,1)S(1)} %collective-permute-done.5.refs_0_), channel_id=1, source_target_pairs={{0,896},{128,0},{256,128},{384,256},{512,384},{640,512},{768,640},... | collective-permute-start | bytes 688136 | tf_op jit(solution)/shard_map/ppermute | solution.py:210
  115.4 3.3 %collective-permute-start.3 = (bf16[128,896]{1,0:T(8,128)(2,1)S(1)}, bf16[128,896]{1,0:T(8,128)(2,1)S(1)}, u32[]{:S(2)}, u32[]{:S(2)}) collective-permute-start(bf16[128,896]{1,0:T(8,128)(2,1)S(1)} %collective-permute-done.2.refs_0_), channel_id=1, source_target_pairs={{0,128},{128,256},{256,384},{384,512},{512,640},{640,768},{768,896... | collective-permute-start | bytes 688136 | tf_op jit(solution)/shard_map/ppermute | solution.py:207
  118.8 0.3 gate_up_step.8
  119.1 0.3 gate_up_step.9
  119.4 0.3 gate_up_step.10
  119.7 0.3 gate_up_step.11
  120.0 0.3 gate_up_step.12
  120.3 0.3 gate_up_step.13
  120.6 0.3 collective-permute-done.6.refs_0_
  120.8 0.3 gate_up_step.14
  121.1 3.5 %collective-permute-done.3.refs_0_ = bf16[128,896]{1,0:T(8,128)(2,1)S(1)} collective-permute-done((bf16[128,896]{1,0:T(8,128)(2,1)S(1)}, bf16[128,896]{1,0:T(8,128)(2,1)S(1)}, u32[]{:S(2)}, u32[]{:S(2)}) %collective-permute-start.3) | collective-permute-done | bytes 229408 | tf_op jit(solution)/shard_map/ppermute | solution.py:207
  124.6 1.0 gate_up_step.15
  125.6 3.5 %all-to-all-start.2 = ((bf16[8,128,128]{2,1,0:T(8,128)(2,1)}), bf16[8,128,128]{2,1,0:T(8,128)(2,1)S(1)}, u32[]{:S(2)}, u32[]{:S(2)}) async-start(bf16[8,128,128]{2,1,0:T(8,128)(2,1)} %gate_up_step.15), calls=%async_computation.2 | async-start | bytes 524288 | tf_op jit(solution)/shard_map/all_to_all | solution.py:17
  129.1 10.4 %all-to-all-done.2.hid_ref = bf16[8,128,128]{2,1,0:T(8,128)(2,1)S(1)} async-done(((bf16[8,128,128]{2,1,0:T(8,128)(2,1)}), bf16[8,128,128]{2,1,0:T(8,128)(2,1)S(1)}, u32[]{:S(2)}, u32[]{:S(2)}) %all-to-all-start.2) | async-done | bytes 262176 | tf_op jit(solution)/shard_map/all_to_all | solution.py:17
  139.5 1.8 down_product.1
  141.3 0.7 reshape.46
  142.0 6.7 %all-to-all-start.3 = ((bf16[32,4,896]{2,1,0:T(4,128)(2,1)}), bf16[32,4,896]{2,1,0:T(4,128)(2,1)S(1)}, u32[]{:S(2)}, u32[]{:S(2)}) async-start(bf16[32,4,896]{2,1,0:T(4,128)(2,1)} %reshape.46), calls=%async_computation.3 | async-start | bytes 458752 | tf_op jit(solution)/shard_map/all_to_all | solution.py:17
  148.8 21.3 %all-to-all-done.3 = bf16[32,4,896]{2,1,0:T(4,128)(2,1)S(1)} async-done(((bf16[32,4,896]{2,1,0:T(4,128)(2,1)}), bf16[32,4,896]{2,1,0:T(4,128)(2,1)S(1)}, u32[]{:S(2)}, u32[]{:S(2)}) %all-to-all-start.3) | async-done | bytes 229408 | tf_op jit(solution)/shard_map/all_to_all | solution.py:17
  170.1 0.3 fusion
  170.5 13.7 %all_to_all.26 = bf16[16,4,896]{2,1,0:T(4,128)(2,1)S(1)} all-to-all(bf16[16,4,896]{2,1,0:T(4,128)(2,1)S(1)} %reshape.47), channel_id=1, replica_groups=mesh['y'=8,'xh'=2,'z'=16,'core'=2,'dp'=2] {'y','xh'}, dimensions={0} | all-to-all | bytes 229376 | tf_op jit(solution)/shard_map/all_to_all | solution.py:17
  184.2 0.1 bitcast_reduce_fusion
  184.4 0.6 copy-done.9
  (38 shorter events, 0.3 us)
Async XLA Ops:
  0.0 0.8 copy-start.2
  1.5 19.8 %all-to-all-start = ((bf16[16,4,896]{2,1,0:T(4,128)(2,1)}), bf16[16,4,896]{2,1,0:T(4,128)(2,1)S(1)}, u32[]{:S(2)}, u32[]{:S(2)}) async-start(bf16[16,4,896]{2,1,0:T(4,128)(2,1)} %in_columns.1), calls=%async_computation | async-start | bytes 229376 | tf_op jit(solution)/shard_map/all_to_all | solution.py:17
  61.9 56.8 %copy-start.1 = (bf16[1,7168,128]{2,1,0:T(8,128)(2,1)S(1)}, bf16[1,7168,128]{2,1,0:T(8,128)(2,1)}, u32[]{:S(2)}) copy-start(bf16[1,7168,128]{2,1,0:T(8,128)(2,1)} %param.10) | copy-start | bytes 5505028
  62.0 56.8 %copy-start = (bf16[1,7168,128]{2,1,0:T(8,128)(2,1)S(1)}, bf16[1,7168,128]{2,1,0:T(8,128)(2,1)}, u32[]{:S(2)}) copy-start(bf16[1,7168,128]{2,1,0:T(8,128)(2,1)} %param.9) | copy-start | bytes 5505028
  62.0 10.0 %collective-permute-start = (bf16[128,896]{1,0:T(8,128)(2,1)S(1)}, bf16[128,896]{1,0:T(8,128)(2,1)S(1)}, u32[]{:S(2)}, u32[]{:S(2)}) collective-permute-start(bf16[128,896]{1,0:T(8,128)(2,1)S(1)} %reshape.45.refs_0_), channel_id=1, source_target_pairs={{0,128},{128,256},{256,384},{384,512},{512,640},{640,768},{768,896... | collective-permute-start | bytes 688136 | tf_op jit(solution)/shard_map/ppermute | solution.py:207
  64.6 25.2 %collective-permute-start.4 = (bf16[128,896]{1,0:T(8,128)(2,1)S(1)}, bf16[128,896]{1,0:T(8,128)(2,1)S(1)}, u32[]{:S(2)}, u32[]{:S(2)}) collective-permute-start(bf16[128,896]{1,0:T(8,128)(2,1)S(1)} %reshape.45.refs_0_), channel_id=1, source_target_pairs={{0,896},{128,0},{256,128},{384,256},{512,384},{640,512},{768,640},... | collective-permute-start | bytes 688136 | tf_op jit(solution)/shard_map/ppermute | solution.py:210
  72.1 21.6 %collective-permute-start.1 = (bf16[128,896]{1,0:T(8,128)(2,1)S(1)}, bf16[128,896]{1,0:T(8,128)(2,1)S(1)}, u32[]{:S(2)}, u32[]{:S(2)}) collective-permute-start(bf16[128,896]{1,0:T(8,128)(2,1)S(1)} %collective-permute-done.refs_0_), channel_id=1, source_target_pairs={{0,128},{128,256},{256,384},{384,512},{512,640},{640,768},{768,896... | collective-permute-start | bytes 688136 | tf_op jit(solution)/shard_map/ppermute | solution.py:207
  74.0 11.9 %collective-permute-start.10 = (bf16[64,896]{1,0:T(8,128)(2,1)S(1)}, bf16[64,896]{1,0:T(8,128)(2,1)S(1)}, u32[]{:S(2)}, u32[]{:S(2)}) collective-permute-start(bf16[64,896]{1,0:T(8,128)(2,1)S(1)} %get-tuple-element.42), channel_id=1, source_target_pairs={{0,512},{1,513},{128,640},{129,641},{256,768},{257,769},{384,896},... | collective-permute-start | bytes 344072 | tf_op jit(solution)/shard_map/ppermute | solution.py:230
  76.8 18.9 %collective-permute-start.7 = (bf16[128,896]{1,0:T(8,128)(2,1)S(1)}, bf16[128,896]{1,0:T(8,128)(2,1)S(1)}, u32[]{:S(2)}, u32[]{:S(2)}) collective-permute-start(bf16[128,896]{1,0:T(8,128)(2,1)S(1)} %get-tuple-element.39), channel_id=1, source_target_pairs={{0,128},{1,897},{128,256},{129,1},{256,384},{257,129},{384,512},{3... | collective-permute-start | bytes 688136 | tf_op jit(solution)/shard_map/ppermute | solution.py:230
  81.8 17.8 %collective-permute-start.8 = (bf16[128,896]{1,0:T(8,128)(2,1)S(1)}, bf16[128,896]{1,0:T(8,128)(2,1)S(1)}, u32[]{:S(2)}, u32[]{:S(2)}) collective-permute-start(bf16[128,896]{1,0:T(8,128)(2,1)S(1)} %get-tuple-element.40), channel_id=1, source_target_pairs={{0,256},{1,769},{128,384},{129,897},{256,512},{257,1},{384,640},{3... | collective-permute-start | bytes 688136 | tf_op jit(solution)/shard_map/ppermute | solution.py:230
  85.9 17.4 %copy-start.6 = (bf16[64,896]{1,0:T(8,128)(2,1)}, bf16[64,896]{1,0:T(8,128)(2,1)S(1)}, u32[]{:S(2)}) copy-start(bf16[64,896]{1,0:T(8,128)(2,1)S(1)} %collective-permute-done.10.refs_3_) | copy-start | bytes 344068
  85.9 17.4 %collective-permute-start.9 = (bf16[128,896]{1,0:T(8,128)(2,1)S(1)}, bf16[128,896]{1,0:T(8,128)(2,1)S(1)}, u32[]{:S(2)}, u32[]{:S(2)}) collective-permute-start(bf16[128,896]{1,0:T(8,128)(2,1)S(1)} %get-tuple-element.41), channel_id=1, source_target_pairs={{0,640},{1,385},{128,768},{129,513},{256,896},{257,641},{384,0},{3... | collective-permute-start | bytes 688136 | tf_op jit(solution)/shard_map/ppermute | solution.py:230
  89.8 23.1 %collective-permute-start.5 = (bf16[128,896]{1,0:T(8,128)(2,1)S(1)}, bf16[128,896]{1,0:T(8,128)(2,1)S(1)}, u32[]{:S(2)}, u32[]{:S(2)}) collective-permute-start(bf16[128,896]{1,0:T(8,128)(2,1)S(1)} %collective-permute-done.4.refs_0_), channel_id=1, source_target_pairs={{0,896},{128,0},{256,128},{384,256},{512,384},{640,512},{768,640},... | collective-permute-start | bytes 688136 | tf_op jit(solution)/shard_map/ppermute | solution.py:210
  93.7 21.7 %collective-permute-start.2 = (bf16[128,896]{1,0:T(8,128)(2,1)S(1)}, bf16[128,896]{1,0:T(8,128)(2,1)S(1)}, u32[]{:S(2)}, u32[]{:S(2)}) collective-permute-start(bf16[128,896]{1,0:T(8,128)(2,1)S(1)} %collective-permute-done.1.refs_0_), channel_id=1, source_target_pairs={{0,128},{128,256},{256,384},{384,512},{512,640},{640,768},{768,896... | collective-permute-start | bytes 688136 | tf_op jit(solution)/shard_map/ppermute | solution.py:207
  95.7 7.7 %copy-start.3 = (bf16[128,896]{1,0:T(8,128)(2,1)}, bf16[128,896]{1,0:T(8,128)(2,1)S(1)}, u32[]{:S(2)}) copy-start(bf16[128,896]{1,0:T(8,128)(2,1)S(1)} %collective-permute-done.7.refs_0_) | copy-start | bytes 688132
  99.7 3.6 %copy-start.4 = (bf16[128,896]{1,0:T(8,128)(2,1)}, bf16[128,896]{1,0:T(8,128)(2,1)S(1)}, u32[]{:S(2)}) copy-start(bf16[128,896]{1,0:T(8,128)(2,1)S(1)} %collective-permute-done.8.refs_1_) | copy-start | bytes 688132
  103.3 0.7 copy-start.5
  105.3 23.8 %collective-permute-start.11 = (bf16[448,896]{1,0:T(8,128)(2,1)S(1)}, bf16[448,896]{1,0:T(8,128)(2,1)}, u32[]{:S(2)}, u32[]{:S(2)}) collective-permute-start(bf16[448,896]{1,0:T(8,128)(2,1)S(1)} %stacked.1.mine_ref), channel_id=1, source_target_pairs={{0,1},{1,0},{2,3},{3,2},{4,5},{5,4},{6,7},{7,6},{8,9},{9,8},{10,11... | collective-permute-start | bytes 2408456 | tf_op jit(solution)/shard_map/ppermute | solution.py:232
  112.9 7.9 %collective-permute-start.6 = (bf16[128,896]{1,0:T(8,128)(2,1)S(1)}, bf16[128,896]{1,0:T(8,128)(2,1)S(1)}, u32[]{:S(2)}, u32[]{:S(2)}) collective-permute-start(bf16[128,896]{1,0:T(8,128)(2,1)S(1)} %collective-permute-done.5.refs_0_), channel_id=1, source_target_pairs={{0,896},{128,0},{256,128},{384,256},{512,384},{640,512},{768,640},... | collective-permute-start | bytes 688136 | tf_op jit(solution)/shard_map/ppermute | solution.py:210
  115.4 9.1 %collective-permute-start.3 = (bf16[128,896]{1,0:T(8,128)(2,1)S(1)}, bf16[128,896]{1,0:T(8,128)(2,1)S(1)}, u32[]{:S(2)}, u32[]{:S(2)}) collective-permute-start(bf16[128,896]{1,0:T(8,128)(2,1)S(1)} %collective-permute-done.2.refs_0_), channel_id=1, source_target_pairs={{0,128},{128,256},{256,384},{384,512},{512,640},{640,768},{768,896... | collective-permute-start | bytes 688136 | tf_op jit(solution)/shard_map/ppermute | solution.py:207
  125.6 23.2 %copy-start.7 = (s32[1,64,8]{1,2,0:T(8,128)S(1)}, s32[1,64,8]{1,2,0:T(8,128)}, u32[]{:S(2)}) copy-start(s32[1,64,8]{1,2,0:T(8,128)} %param.8) | copy-start | bytes 6148
  125.6 23.2 %copy-start.8 = (s32[1,64,8]{1,2,0:T(8,128)S(1)}, s32[1,64,8]{1,2,0:T(8,128)}, u32[]{:S(2)}) copy-start(s32[1,64,8]{1,2,0:T(8,128)} %param.7) | copy-start | bytes 6148
  125.6 13.9 %all-to-all-start.2 = ((bf16[8,128,128]{2,1,0:T(8,128)(2,1)}), bf16[8,128,128]{2,1,0:T(8,128)(2,1)S(1)}, u32[]{:S(2)}, u32[]{:S(2)}) async-start(bf16[8,128,128]{2,1,0:T(8,128)(2,1)} %gate_up_step.15), calls=%async_computation.2 | async-start | bytes 524288 | tf_op jit(solution)/shard_map/all_to_all | solution.py:17
  142.0 28.1 %all-to-all-start.3 = ((bf16[32,4,896]{2,1,0:T(4,128)(2,1)}), bf16[32,4,896]{2,1,0:T(4,128)(2,1)S(1)}, u32[]{:S(2)}, u32[]{:S(2)}) async-start(bf16[32,4,896]{2,1,0:T(4,128)(2,1)} %reshape.46), calls=%async_computation.3 | async-start | bytes 458752 | tf_op jit(solution)/shard_map/all_to_all | solution.py:17
  184.4 0.6 copy-start.9

commit v3 on v2

--- a/solution.py
+++ b/solution.py
@@ -182,16 +182,17 @@
     )(*(in_vmem(x) for x in (shard, gate, up, *(sums or ()))))
 
 
-def routing(expert_ids, gate_codes, experts, capacity):
-    window = jnp.arange(experts, dtype=jnp.int32)
+def routing(expert_ids, gate_codes, window, capacity):
     hits = expert_ids[..., None] == window
     member = jnp.any(hits, axis=-2)
     codes = gate_codes.astype(jnp.float32)
     gates = 2.5 * codes / jnp.sum(codes, axis=-1, keepdims=True)
     weight = jnp.sum(jnp.where(hits, gates[..., None], jnp.float32(0.0)), axis=-2)
-    tokens = expert_ids.shape[0]
+    tokens = expert_ids.shape[1]
     before = jnp.tril(jnp.ones((tokens, tokens), jnp.bfloat16), -1)
-    rank = jnp.dot(before, member.astype(jnp.bfloat16), preferred_element_type=jnp.float32)
+    rank = jnp.einsum(
+        "ut,cte->cue", before, member.astype(jnp.bfloat16), preferred_element_type=jnp.float32
+    )
     slots = jnp.arange(capacity, dtype=jnp.float32)
     place = member[..., None] & (rank[..., None] == slots)
     return place, weight
@@ -214,11 +215,16 @@
 
 def per_device(tokens, expert_ids, gate_codes, w_gate, w_up, w_down):
     ny, nh = lax.axis_size("y"), lax.axis_size("xh")
-    experts = lax.axis_size(EXPERT)
+    nz, nc = lax.axis_size("z"), lax.axis_size("core")
+    core = lax.axis_index("core")
     own, width = tokens.shape[1], tokens.shape[2]
     cols = width // ny
 
-    toks = exchange(in_columns(tokens[0], ny, nh), GROUP)
+    mine = jnp.stack([expert_ids[0], gate_codes[0]])
+    other = lax.ppermute(mine, "core", [(0, 1), (1, 0)])
+    both = jnp.where(core == 0, jnp.stack([mine, other]), jnp.stack([other, mine]))
+    toks = exchange(in_columns(tokens[0], ny, nh * nc), (*GROUP, "core"))
+    toks = jnp.moveaxis(toks.reshape(ny * nh, nc, own, cols), 1, 0)
     own_block, *blocks = cut_blocks(w_down[0])
     sides = lax.axis_size("dp")
     for k in range(1, ny // 2 + 1):
@@ -231,17 +237,17 @@
     mine = stacked(blocks)
     others = lax.ppermute(mine, "dp", [(0, 1), (1, 0)])
 
-    place, weight = routing(expert_ids[0], gate_codes[0], experts, CAPG)
+    window = nc * jnp.arange(nz, dtype=jnp.int32) + core
+    place, weight = routing(both[:, 0], both[:, 1], window, CAPG)
     mix = jnp.where(place, weight[..., None], jnp.float32(0.0))
     rows = jnp.einsum(
-        "tej,td->ejd",
+        "ctej,ctd->ecjd",
         place.astype(jnp.bfloat16),
-        toks.reshape(ny * nh * own, cols),
+        toks.reshape(nc, ny * nh * own, cols),
         preferred_element_type=jnp.float32,
     ).astype(jnp.bfloat16)
-    got = exchange(rows, EXPERT)
-    sets = got.shape[0]
-    count = sets * CAPG
+    got = exchange(rows, "z")
+    count = nz * nc * CAPG
     sums = None
     shards = around(got.reshape(count, cols), "y")
     for step, shard in shards:
@@ -249,16 +255,18 @@
         sums = gate_up_step(sums, shard, w_gate[0], w_up[0], step, "y", last)
     hiddens = exchange(sums, "y")
     outs = down_product(hiddens, own_block, mine, others)
-    back = exchange(outs.reshape(sets, CAPG, cols), EXPERT)
+    back = exchange(outs.reshape(nz, nc, CAPG, cols), "z")
     mixed = jnp.einsum(
-        "tej,ejc->tc",
+        "ctej,ecjd->tcd",
         mix,
         back.astype(jnp.float32),
         precision=lax.Precision.HIGHEST,
         preferred_element_type=jnp.float32,
     )
-    home = exchange(mixed.astype(jnp.bfloat16).reshape(ny * nh, own, cols), GROUP)
-    home = home.reshape(ny, nh, own, cols).astype(jnp.float32)
+    mixed = mixed.astype(jnp.bfloat16).reshape(ny * nh, own, nc, cols)
+    mixed = jnp.moveaxis(mixed, 2, 1).reshape(ny * nh * nc, own, cols)
+    home = exchange(mixed, (*GROUP, "core"))
+    home = home.reshape(ny, nh * nc, own, cols).astype(jnp.float32)
     home = jnp.sum(home, axis=1).astype(jnp.bfloat16)
     return jnp.concatenate([home[i] for i in range(ny)], axis=1)[None]
 

time: 186 us -> 185 us (level)
  the two profiles are of different devices: /device:TPU:2 before, /device:TPU:1 now
where the time goes in v3:
time: 185 us; the launch traced here: 184 us
  starting transfers between devices  81.9 us (44%)
  blocking collectives  49 us (26%)
  waiting for transfers between devices  38.7 us (21%)
  Pallas kernels  8.1 us (4%)
  local copies, waits for them, and re-layouts  4.78 us (3%)
    all_to_all x2, blocking collectives, exchange(): return lax.all_to_all(parts, axes, 0, 0, tiled=True)  49 us
    all_to_all x3, waiting for transfers between devices, exchange(): return lax.all_to_all(parts, axes, 0, 0, tiled=True)  33.6 us
    all_to_all x3, starting transfers between devices, exchange(): return lax.all_to_all(parts, axes, 0, 0, tiled=True)  22.6 us
    ppermute x1, starting transfers between devices, per_device(): other = lax.ppermute(mine, 'core', [(0, 1), (1, 0)])  16 us
    ppermute x3, starting transfers between devices, around(): b = lax.ppermute(b, axis, down)  15 us
    ppermute x4, starting transfers between devices, per_device(): blocks[k - 1] = lax.ppermute(blocks[k - 1], ('y', 'dp'), pairs)  14.1 us
    ppermute x4, starting transfers between devices, around(): a = lax.ppermute(a, axis, up)  11.3 us
    ppermute x4, waiting for transfers between devices, per_device(): blocks[k - 1] = lax.ppermute(blocks[k - 1], ('y', 'dp'), pairs)  4.16 us
  transfers between devices with their start and end apart: 16, of which 7 were waited for; matrix products, arithmetic and copies ran while one was open for 0% of the time, Pallas kernels for 3%

profile of v3, /device:TPU:1, one launch (start us, length us, event | category | flops | bytes accessed | tf_op | source)
XLA Modules:
  0.0 184.0 jit_solution(3902323567685721932)
XLA Ops:
  0.0 0.7 constant_dynamic-update-slice_fusion.1
  0.7 0.7 constant_dynamic-update-slice_fusion
  1.4 16.0 %collective-permute-start = (s32[2,64,8]{1,2,0:T(8,128)S(1)}, s32[2,64,8]{1,2,0:T(8,128)S(1)}, u32[]{:S(2)}, u32[]{:S(2)}) collective-permute-start(s32[2,64,8]{1,2,0:T(8,128)S(1)} %constant_dynamic-update-slice_fusion), channel_id=1, source_target_pairs={{0,2},{2,0},{1,3},{3,1},{4,6},{6,4},{5,7},{7,5},{8,10},{10,8},{9,1... | collective-permute-start | bytes 12296 | tf_op jit(solution)/shard_map/ppermute | solution.py:224
  17.4 0.8 copy-done.2
  18.2 0.7 in_columns.1
  18.9 3.7 %all-to-all-start = ((bf16[32,4,896]{2,1,0:T(4,128)(2,1)}), bf16[32,4,896]{2,1,0:T(4,128)(2,1)S(1)}, u32[]{:S(2)}, u32[]{:S(2)}) async-start(bf16[32,4,896]{2,1,0:T(4,128)(2,1)} %in_columns.1), calls=%async_computation | async-start | bytes 458752 | tf_op jit(solution)/shard_map/all_to_all | solution.py:17
  22.6 0.1 compare_reduce_fusion
  22.7 0.2 convolution_bitcast_fusion.1
  22.9 11.9 %all-to-all-done = bf16[32,4,896]{2,1,0:T(4,128)(2,1)S(1)} async-done(((bf16[32,4,896]{2,1,0:T(4,128)(2,1)}), bf16[32,4,896]{2,1,0:T(4,128)(2,1)S(1)}, u32[]{:S(2)}, u32[]{:S(2)}) %all-to-all-start) | async-done | bytes 229408 | tf_op jit(solution)/shard_map/all_to_all | solution.py:17
  35.0 0.2 fusion.1
  35.2 0.1 copy.25
  35.3 25.3 %all_to_all.25 = bf16[16,2,4,896]{3,2,1,0:T(4,128)(2,1)S(1)} all-to-all(bf16[16,2,4,896]{3,2,1,0:T(4,128)(2,1)S(1)} %copy.25), channel_id=1, replica_groups=mesh['y'=8,'xh'=2,'z'=16,'core'=2,'dp'=2] {'z'}, dimensions={0} | all-to-all | bytes 458752 | tf_op jit(solution)/shard_map/all_to_all | solution.py:17
  60.6 2.2 %collective-permute-start.1 = (bf16[128,896]{1,0:T(8,128)(2,1)S(1)}, bf16[128,896]{1,0:T(8,128)(2,1)S(1)}, u32[]{:S(2)}, u32[]{:S(2)}) collective-permute-start(bf16[128,896]{1,0:T(8,128)(2,1)S(1)} %reshape.43.refs_0_), channel_id=1, source_target_pairs={{0,128},{128,256},{256,384},{384,512},{512,640},{640,768},{768,896... | collective-permute-start | bytes 688136 | tf_op jit(solution)/shard_map/ppermute | solution.py:208
  62.8 4.6 %collective-permute-start.5 = (bf16[128,896]{1,0:T(8,128)(2,1)S(1)}, bf16[128,896]{1,0:T(8,128)(2,1)S(1)}, u32[]{:S(2)}, u32[]{:S(2)}) collective-permute-start(bf16[128,896]{1,0:T(8,128)(2,1)S(1)} %reshape.43.refs_0_), channel_id=1, source_target_pairs={{0,896},{128,0},{256,128},{384,256},{512,384},{640,512},{768,640},... | collective-permute-start | bytes 688136 | tf_op jit(solution)/shard_map/ppermute | solution.py:211
  67.4 1.4 cut_blocks.1
  68.9 1.9 %collective-permute-start.2 = (bf16[128,896]{1,0:T(8,128)(2,1)S(1)}, bf16[128,896]{1,0:T(8,128)(2,1)S(1)}, u32[]{:S(2)}, u32[]{:S(2)}) collective-permute-start(bf16[128,896]{1,0:T(8,128)(2,1)S(1)} %collective-permute-done.1.refs_0_), channel_id=1, source_target_pairs={{0,128},{128,256},{256,384},{384,512},{512,640},{640,768},{768,896... | collective-permute-start | bytes 688136 | tf_op jit(solution)/shard_map/ppermute | solution.py:208
  70.8 3.6 %collective-permute-start.11 = (bf16[64,896]{1,0:T(8,128)(2,1)S(1)}, bf16[64,896]{1,0:T(8,128)(2,1)S(1)}, u32[]{:S(2)}, u32[]{:S(2)}) collective-permute-start(bf16[64,896]{1,0:T(8,128)(2,1)S(1)} %get-tuple-element.42), channel_id=1, source_target_pairs={{0,512},{1,513},{128,640},{129,641},{256,768},{257,769},{384,896},... | collective-permute-start | bytes 344072 | tf_op jit(solution)/shard_map/ppermute | solution.py:236
  74.4 1.9 %collective-permute-start.8 = (bf16[128,896]{1,0:T(8,128)(2,1)S(1)}, bf16[128,896]{1,0:T(8,128)(2,1)S(1)}, u32[]{:S(2)}, u32[]{:S(2)}) collective-permute-start(bf16[128,896]{1,0:T(8,128)(2,1)S(1)} %get-tuple-element.39), channel_id=1, source_target_pairs={{0,128},{1,897},{128,256},{129,1},{256,384},{257,129},{384,512},{3... | collective-permute-start | bytes 688136 | tf_op jit(solution)/shard_map/ppermute | solution.py:236
  76.3 6.2 %collective-permute-start.9 = (bf16[128,896]{1,0:T(8,128)(2,1)S(1)}, bf16[128,896]{1,0:T(8,128)(2,1)S(1)}, u32[]{:S(2)}, u32[]{:S(2)}) collective-permute-start(bf16[128,896]{1,0:T(8,128)(2,1)S(1)} %get-tuple-element.40), channel_id=1, source_target_pairs={{0,256},{1,769},{128,384},{129,897},{256,512},{257,1},{384,640},{3... | collective-permute-start | bytes 688136 | tf_op jit(solution)/shard_map/ppermute | solution.py:236
  82.5 2.4 %collective-permute-start.10 = (bf16[128,896]{1,0:T(8,128)(2,1)S(1)}, bf16[128,896]{1,0:T(8,128)(2,1)S(1)}, u32[]{:S(2)}, u32[]{:S(2)}) collective-permute-start(bf16[128,896]{1,0:T(8,128)(2,1)S(1)} %get-tuple-element.41), channel_id=1, source_target_pairs={{0,640},{1,385},{128,768},{129,513},{256,896},{257,641},{384,0},{3... | collective-permute-start | bytes 688136 | tf_op jit(solution)/shard_map/ppermute | solution.py:236
  84.9 3.4 %collective-permute-start.6 = (bf16[128,896]{1,0:T(8,128)(2,1)S(1)}, bf16[128,896]{1,0:T(8,128)(2,1)S(1)}, u32[]{:S(2)}, u32[]{:S(2)}) collective-permute-start(bf16[128,896]{1,0:T(8,128)(2,1)S(1)} %collective-permute-done.5.refs_0_), channel_id=1, source_target_pairs={{0,896},{128,0},{256,128},{384,256},{512,384},{640,512},{768,640},... | collective-permute-start | bytes 688136 | tf_op jit(solution)/shard_map/ppermute | solution.py:211
  88.3 1.9 %collective-permute-start.3 = (bf16[128,896]{1,0:T(8,128)(2,1)S(1)}, bf16[128,896]{1,0:T(8,128)(2,1)S(1)}, u32[]{:S(2)}, u32[]{:S(2)}) collective-permute-start(bf16[128,896]{1,0:T(8,128)(2,1)S(1)} %collective-permute-done.2.refs_0_), channel_id=1, source_target_pairs={{0,128},{128,256},{256,384},{384,512},{512,640},{640,768},{768,896... | collective-permute-start | bytes 688136 | tf_op jit(solution)/shard_map/ppermute | solution.py:208
  90.3 1.6 collective-permute-done.9.refs_1_
  91.9 2.5 %collective-permute-done.10.refs_2_ = bf16[128,896]{1,0:T(8,128)(2,1)S(1)} collective-permute-done((bf16[128,896]{1,0:T(8,128)(2,1)S(1)}, bf16[128,896]{1,0:T(8,128)(2,1)S(1)}, u32[]{:S(2)}, u32[]{:S(2)}) %collective-permute-start.10) | collective-permute-done | bytes 229408 | tf_op jit(solution)/shard_map/ppermute | solution.py:236
  94.4 0.7 copy-done.5
  95.1 1.3 stacked.1.mine_ref
  96.4 3.0 %collective-permute-start.12 = (bf16[448,896]{1,0:T(8,128)(2,1)S(1)}, bf16[448,896]{1,0:T(8,128)(2,1)}, u32[]{:S(2)}, u32[]{:S(2)}) collective-permute-start(bf16[448,896]{1,0:T(8,128)(2,1)S(1)} %stacked.1.mine_ref), channel_id=1, source_target_pairs={{0,1},{1,0},{2,3},{3,2},{4,5},{5,4},{6,7},{7,6},{8,9},{9,8},{10,11... | collective-permute-start | bytes 2408456 | tf_op jit(solution)/shard_map/ppermute | solution.py:238
  99.4 7.0 %collective-permute-start.7 = (bf16[128,896]{1,0:T(8,128)(2,1)S(1)}, bf16[128,896]{1,0:T(8,128)(2,1)S(1)}, u32[]{:S(2)}, u32[]{:S(2)}) collective-permute-start(bf16[128,896]{1,0:T(8,128)(2,1)S(1)} %collective-permute-done.6.refs_0_), channel_id=1, source_target_pairs={{0,896},{128,0},{256,128},{384,256},{512,384},{640,512},{768,640},... | collective-permute-start | bytes 688136 | tf_op jit(solution)/shard_map/ppermute | solution.py:211
  106.5 5.2 %collective-permute-start.4 = (bf16[128,896]{1,0:T(8,128)(2,1)S(1)}, bf16[128,896]{1,0:T(8,128)(2,1)S(1)}, u32[]{:S(2)}, u32[]{:S(2)}) collective-permute-start(bf16[128,896]{1,0:T(8,128)(2,1)S(1)} %collective-permute-done.3.refs_0_), channel_id=1, source_target_pairs={{0,128},{128,256},{256,384},{384,512},{512,640},{640,768},{768,896... | collective-permute-start | bytes 688136 | tf_op jit(solution)/shard_map/ppermute | solution.py:208
  111.7 0.3 gate_up_step.8
  112.0 0.3 gate_up_step.9
  112.3 0.3 gate_up_step.10
  112.6 0.3 gate_up_step.11
  112.9 0.3 gate_up_step.12
  113.2 0.3 gate_up_step.13
  113.5 0.3 gate_up_step.14
  113.8 0.9 collective-permute-done.4.refs_0_
  114.7 1.0 gate_up_step.15
  115.7 4.8 %all-to-all-start.2 = ((bf16[8,128,128]{2,1,0:T(8,128)(2,1)}), bf16[8,128,128]{2,1,0:T(8,128)(2,1)S(1)}, u32[]{:S(2)}, u32[]{:S(2)}) async-start(bf16[8,128,128]{2,1,0:T(8,128)(2,1)} %gate_up_step.15), calls=%async_computation.2 | async-start | bytes 524288 | tf_op jit(solution)/shard_map/all_to_all | solution.py:17
  120.4 9.3 %all-to-all-done.2.hid_ref = bf16[8,128,128]{2,1,0:T(8,128)(2,1)S(1)} async-done(((bf16[8,128,128]{2,1,0:T(8,128)(2,1)}), bf16[8,128,128]{2,1,0:T(8,128)(2,1)S(1)}, u32[]{:S(2)}, u32[]{:S(2)}) %all-to-all-start.2) | async-done | bytes 262176 | tf_op jit(solution)/shard_map/all_to_all | solution.py:17
  129.7 1.8 down_product.1
  131.5 0.7 reshape.44
  132.3 14.1 %all-to-all-start.3 = ((bf16[16,2,4,896]{3,2,1,0:T(4,128)(2,1)}), bf16[16,2,4,896]{3,2,1,0:T(4,128)(2,1)S(1)}, u32[]{:S(2)}, u32[]{:S(2)}) async-start(bf16[16,2,4,896]{3,2,1,0:T(4,128)(2,1)} %reshape.44), calls=%async_computation.3 | async-start | bytes 458752 | tf_op jit(solution)/shard_map/all_to_all | solution.py:17
  146.5 12.4 %all-to-all-done.3 = bf16[16,2,4,896]{3,2,1,0:T(4,128)(2,1)S(1)} async-done(((bf16[16,2,4,896]{3,2,1,0:T(4,128)(2,1)}), bf16[16,2,4,896]{3,2,1,0:T(4,128)(2,1)S(1)}, u32[]{:S(2)}, u32[]{:S(2)}) %all-to-all-start.3) | async-done | bytes 229408 | tf_op jit(solution)/shard_map/all_to_all | solution.py:17
  158.9 0.4 fusion.2
  159.5 23.7 %all_to_all.26 = bf16[32,4,896]{2,1,0:T(4,128)(2,1)S(1)} all-to-all(bf16[32,4,896]{2,1,0:T(4,128)(2,1)S(1)} %bitcast.92), channel_id=1, replica_groups=mesh['y'=8,'xh'=2,'z'=16,'core'=2,'dp'=2] {'y','xh','core'}, dimensions={0} | all-to-all | bytes 458752 | tf_op jit(solution)/shard_map/all_to_all | solution.py:17
  183.2 0.1 bitcast_reduce_fusion
  183.4 0.6 copy-done.7
  (43 shorter events, 0.7 us)
Async XLA Ops:
  1.4 21.2 %collective-permute-start = (s32[2,64,8]{1,2,0:T(8,128)S(1)}, s32[2,64,8]{1,2,0:T(8,128)S(1)}, u32[]{:S(2)}, u32[]{:S(2)}) collective-permute-start(s32[2,64,8]{1,2,0:T(8,128)S(1)} %constant_dynamic-update-slice_fusion), channel_id=1, source_target_pairs={{0,2},{2,0},{1,3},{3,1},{4,6},{6,4},{5,7},{7,5},{8,10},{10,8},{9,1... | collective-permute-start | bytes 12296 | tf_op jit(solution)/shard_map/ppermute | solution.py:224
  17.4 0.8 copy-start.2
  18.9 15.9 %all-to-all-start = ((bf16[32,4,896]{2,1,0:T(4,128)(2,1)}), bf16[32,4,896]{2,1,0:T(4,128)(2,1)S(1)}, u32[]{:S(2)}, u32[]{:S(2)}) async-start(bf16[32,4,896]{2,1,0:T(4,128)(2,1)} %in_columns.1), calls=%async_computation | async-start | bytes 458752 | tf_op jit(solution)/shard_map/all_to_all | solution.py:17
  60.6 51.1 %copy-start.1 = (bf16[1,7168,128]{2,1,0:T(8,128)(2,1)S(1)}, bf16[1,7168,128]{2,1,0:T(8,128)(2,1)}, u32[]{:S(2)}) copy-start(bf16[1,7168,128]{2,1,0:T(8,128)(2,1)} %param.10) | copy-start | bytes 5505028
  60.6 51.1 %copy-start = (bf16[1,7168,128]{2,1,0:T(8,128)(2,1)S(1)}, bf16[1,7168,128]{2,1,0:T(8,128)(2,1)}, u32[]{:S(2)}) copy-start(bf16[1,7168,128]{2,1,0:T(8,128)(2,1)} %param.9) | copy-start | bytes 5505028
  60.6 8.2 %collective-permute-start.1 = (bf16[128,896]{1,0:T(8,128)(2,1)S(1)}, bf16[128,896]{1,0:T(8,128)(2,1)S(1)}, u32[]{:S(2)}, u32[]{:S(2)}) collective-permute-start(bf16[128,896]{1,0:T(8,128)(2,1)S(1)} %reshape.43.refs_0_), channel_id=1, source_target_pairs={{0,128},{128,256},{256,384},{384,512},{512,640},{640,768},{768,896... | collective-permute-start | bytes 688136 | tf_op jit(solution)/shard_map/ppermute | solution.py:208
  62.8 22.1 %collective-permute-start.5 = (bf16[128,896]{1,0:T(8,128)(2,1)S(1)}, bf16[128,896]{1,0:T(8,128)(2,1)S(1)}, u32[]{:S(2)}, u32[]{:S(2)}) collective-permute-start(bf16[128,896]{1,0:T(8,128)(2,1)S(1)} %reshape.43.refs_0_), channel_id=1, source_target_pairs={{0,896},{128,0},{256,128},{384,256},{512,384},{640,512},{768,640},... | collective-permute-start | bytes 688136 | tf_op jit(solution)/shard_map/ppermute | solution.py:211
  68.9 19.4 %collective-permute-start.2 = (bf16[128,896]{1,0:T(8,128)(2,1)S(1)}, bf16[128,896]{1,0:T(8,128)(2,1)S(1)}, u32[]{:S(2)}, u32[]{:S(2)}) collective-permute-start(bf16[128,896]{1,0:T(8,128)(2,1)S(1)} %collective-permute-done.1.refs_0_), channel_id=1, source_target_pairs={{0,128},{128,256},{256,384},{384,512},{512,640},{640,768},{768,896... | collective-permute-start | bytes 688136 | tf_op jit(solution)/shard_map/ppermute | solution.py:208
  70.8 11.7 %collective-permute-start.11 = (bf16[64,896]{1,0:T(8,128)(2,1)S(1)}, bf16[64,896]{1,0:T(8,128)(2,1)S(1)}, u32[]{:S(2)}, u32[]{:S(2)}) collective-permute-start(bf16[64,896]{1,0:T(8,128)(2,1)S(1)} %get-tuple-element.42), channel_id=1, source_target_pairs={{0,512},{1,513},{128,640},{129,641},{256,768},{257,769},{384,896},... | collective-permute-start | bytes 344072 | tf_op jit(solution)/shard_map/ppermute | solution.py:236
  74.4 15.8 %collective-permute-start.8 = (bf16[128,896]{1,0:T(8,128)(2,1)S(1)}, bf16[128,896]{1,0:T(8,128)(2,1)S(1)}, u32[]{:S(2)}, u32[]{:S(2)}) collective-permute-start(bf16[128,896]{1,0:T(8,128)(2,1)S(1)} %get-tuple-element.39), channel_id=1, source_target_pairs={{0,128},{1,897},{128,256},{129,1},{256,384},{257,129},{384,512},{3... | collective-permute-start | bytes 688136 | tf_op jit(solution)/shard_map/ppermute | solution.py:236
  76.3 15.6 %collective-permute-start.9 = (bf16[128,896]{1,0:T(8,128)(2,1)S(1)}, bf16[128,896]{1,0:T(8,128)(2,1)S(1)}, u32[]{:S(2)}, u32[]{:S(2)}) collective-permute-start(bf16[128,896]{1,0:T(8,128)(2,1)S(1)} %get-tuple-element.40), channel_id=1, source_target_pairs={{0,256},{1,769},{128,384},{129,897},{256,512},{257,1},{384,640},{3... | collective-permute-start | bytes 688136 | tf_op jit(solution)/shard_map/ppermute | solution.py:236
  82.5 11.9 %copy-start.6 = (bf16[64,896]{1,0:T(8,128)(2,1)}, bf16[64,896]{1,0:T(8,128)(2,1)S(1)}, u32[]{:S(2)}) copy-start(bf16[64,896]{1,0:T(8,128)(2,1)S(1)} %collective-permute-done.11.refs_3_) | copy-start | bytes 344068
  82.5 11.9 %collective-permute-start.10 = (bf16[128,896]{1,0:T(8,128)(2,1)S(1)}, bf16[128,896]{1,0:T(8,128)(2,1)S(1)}, u32[]{:S(2)}, u32[]{:S(2)}) collective-permute-start(bf16[128,896]{1,0:T(8,128)(2,1)S(1)} %get-tuple-element.41), channel_id=1, source_target_pairs={{0,640},{1,385},{128,768},{129,513},{256,896},{257,641},{384,0},{3... | collective-permute-start | bytes 688136 | tf_op jit(solution)/shard_map/ppermute | solution.py:236
  84.9 14.5 %collective-permute-start.6 = (bf16[128,896]{1,0:T(8,128)(2,1)S(1)}, bf16[128,896]{1,0:T(8,128)(2,1)S(1)}, u32[]{:S(2)}, u32[]{:S(2)}) collective-permute-start(bf16[128,896]{1,0:T(8,128)(2,1)S(1)} %collective-permute-done.5.refs_0_), channel_id=1, source_target_pairs={{0,896},{128,0},{256,128},{384,256},{512,384},{640,512},{768,640},... | collective-permute-start | bytes 688136 | tf_op jit(solution)/shard_map/ppermute | solution.py:211
  88.3 18.2 %collective-permute-start.3 = (bf16[128,896]{1,0:T(8,128)(2,1)S(1)}, bf16[128,896]{1,0:T(8,128)(2,1)S(1)}, u32[]{:S(2)}, u32[]{:S(2)}) collective-permute-start(bf16[128,896]{1,0:T(8,128)(2,1)S(1)} %collective-permute-done.2.refs_0_), channel_id=1, source_target_pairs={{0,128},{128,256},{256,384},{384,512},{512,640},{640,768},{768,896... | collective-permute-start | bytes 688136 | tf_op jit(solution)/shard_map/ppermute | solution.py:208
  90.2 4.2 %copy-start.3 = (bf16[128,896]{1,0:T(8,128)(2,1)}, bf16[128,896]{1,0:T(8,128)(2,1)S(1)}, u32[]{:S(2)}) copy-start(bf16[128,896]{1,0:T(8,128)(2,1)S(1)} %collective-permute-done.8.refs_0_) | copy-start | bytes 688132
  91.9 2.5 %copy-start.4 = (bf16[128,896]{1,0:T(8,128)(2,1)}, bf16[128,896]{1,0:T(8,128)(2,1)S(1)}, u32[]{:S(2)}) copy-start(bf16[128,896]{1,0:T(8,128)(2,1)S(1)} %collective-permute-done.9.refs_1_) | copy-start | bytes 688132
  94.4 0.7 copy-start.5
  96.4 24.0 %collective-permute-start.12 = (bf16[448,896]{1,0:T(8,128)(2,1)S(1)}, bf16[448,896]{1,0:T(8,128)(2,1)}, u32[]{:S(2)}, u32[]{:S(2)}) collective-permute-start(bf16[448,896]{1,0:T(8,128)(2,1)S(1)} %stacked.1.mine_ref), channel_id=1, source_target_pairs={{0,1},{1,0},{2,3},{3,2},{4,5},{5,4},{6,7},{7,6},{8,9},{9,8},{10,11... | collective-permute-start | bytes 2408456 | tf_op jit(solution)/shard_map/ppermute | solution.py:238
  99.4 14.1 %collective-permute-start.7 = (bf16[128,896]{1,0:T(8,128)(2,1)S(1)}, bf16[128,896]{1,0:T(8,128)(2,1)S(1)}, u32[]{:S(2)}, u32[]{:S(2)}) collective-permute-start(bf16[128,896]{1,0:T(8,128)(2,1)S(1)} %collective-permute-done.6.refs_0_), channel_id=1, source_target_pairs={{0,896},{128,0},{256,128},{384,256},{512,384},{640,512},{768,640},... | collective-permute-start | bytes 688136 | tf_op jit(solution)/shard_map/ppermute | solution.py:211
  106.5 8.2 %collective-permute-start.4 = (bf16[128,896]{1,0:T(8,128)(2,1)S(1)}, bf16[128,896]{1,0:T(8,128)(2,1)S(1)}, u32[]{:S(2)}, u32[]{:S(2)}) collective-permute-start(bf16[128,896]{1,0:T(8,128)(2,1)S(1)} %collective-permute-done.3.refs_0_), channel_id=1, source_target_pairs={{0,128},{128,256},{256,384},{384,512},{512,640},{640,768},{768,896... | collective-permute-start | bytes 688136 | tf_op jit(solution)/shard_map/ppermute | solution.py:208
  115.7 14.1 %all-to-all-start.2 = ((bf16[8,128,128]{2,1,0:T(8,128)(2,1)}), bf16[8,128,128]{2,1,0:T(8,128)(2,1)S(1)}, u32[]{:S(2)}, u32[]{:S(2)}) async-start(bf16[8,128,128]{2,1,0:T(8,128)(2,1)} %gate_up_step.15), calls=%async_computation.2 | async-start | bytes 524288 | tf_op jit(solution)/shard_map/all_to_all | solution.py:17
  132.3 26.7 %all-to-all-start.3 = ((bf16[16,2,4,896]{3,2,1,0:T(4,128)(2,1)}), bf16[16,2,4,896]{3,2,1,0:T(4,128)(2,1)S(1)}, u32[]{:S(2)}, u32[]{:S(2)}) async-start(bf16[16,2,4,896]{3,2,1,0:T(4,128)(2,1)} %reshape.44), calls=%async_computation.3 | async-start | bytes 458752 | tf_op jit(solution)/shard_map/all_to_all | solution.py:17
  183.4 0.6 copy-start.7

commit v4 on v3

--- a/solution.py
+++ b/solution.py
@@ -189,10 +189,8 @@
     gates = 2.5 * codes / jnp.sum(codes, axis=-1, keepdims=True)
     weight = jnp.sum(jnp.where(hits, gates[..., None], jnp.float32(0.0)), axis=-2)
     tokens = expert_ids.shape[1]
-    before = jnp.tril(jnp.ones((tokens, tokens), jnp.bfloat16), -1)
-    rank = jnp.einsum(
-        "ut,cte->cue", before, member.astype(jnp.bfloat16), preferred_element_type=jnp.float32
-    )
+    before = jnp.tril(jnp.ones((tokens, tokens), jnp.float32), -1)
+    rank = jnp.einsum("ut,cte->cue", before, member.astype(jnp.float32))
     slots = jnp.arange(capacity, dtype=jnp.float32)
     place = member[..., None] & (rank[..., None] == slots)
     return place, weight
@@ -223,8 +221,7 @@
     mine = jnp.stack([expert_ids[0], gate_codes[0]])
     other = lax.ppermute(mine, "core", [(0, 1), (1, 0)])
     both = jnp.where(core == 0, jnp.stack([mine, other]), jnp.stack([other, mine]))
-    toks = exchange(in_columns(tokens[0], ny, nh * nc), (*GROUP, "core"))
-    toks = jnp.moveaxis(toks.reshape(ny * nh, nc, own, cols), 1, 0)
+    toks = exchange(in_columns(tokens[0], ny, nh), GROUP)
     own_block, *blocks = cut_blocks(w_down[0])
     sides = lax.axis_size("dp")
     for k in range(1, ny // 2 + 1):
@@ -237,16 +234,18 @@
     mine = stacked(blocks)
     others = lax.ppermute(mine, "dp", [(0, 1), (1, 0)])
 
+    experts = jnp.arange(nz * nc, dtype=jnp.int32)
+    place, _ = routing(expert_ids, gate_codes, experts, CAPG)
+    rows = jnp.einsum(
+        "tej,td->ejd",
+        place[0].astype(jnp.bfloat16),
+        toks.reshape(ny * nh * own, cols),
+        preferred_element_type=jnp.float32,
+    ).astype(jnp.bfloat16)
+    got = exchange(rows, EXPERT)
     window = nc * jnp.arange(nz, dtype=jnp.int32) + core
     place, weight = routing(both[:, 0], both[:, 1], window, CAPG)
     mix = jnp.where(place, weight[..., None], jnp.float32(0.0))
-    rows = jnp.einsum(
-        "ctej,ctd->ecjd",
-        place.astype(jnp.bfloat16),
-        toks.reshape(nc, ny * nh * own, cols),
-        preferred_element_type=jnp.float32,
-    ).astype(jnp.bfloat16)
-    got = exchange(rows, "z")
     count = nz * nc * CAPG
     sums = None
     shards = around(got.reshape(count, cols), "y")

time: 185 us -> 184 us (level)
  blocking collectives: 49 us -> 65.2 us
  starting transfers between devices: 81.9 us -> 66.7 us
    all_to_all x2, blocking collectives: 49 us -> 65.2 us  [exchange(): return lax.all_to_all(parts, axes, 0, 0, tiled=True)]
    all_to_all x3, waiting for transfers between devices: 33.6 us -> 22 us  [exchange(): return lax.all_to_all(parts, axes, 0, 0, tiled=True)]
    ppermute x1, starting transfers between devices: 16 us -> 7.53 us  [per_device(): other = lax.ppermute(mine, 'core', [(0, 1), (1, 0)])]
    ppermute x4, waiting for transfers between devices: 0.95 us -> 6.96 us  [around(): a = lax.ppermute(a, axis, up)]
    ppermute x4, starting transfers between devices: 11.3 us -> 8.25 us  [around(): a = lax.ppermute(a, axis, up)]
    all_to_all x3, starting transfers between devices: 22.6 us -> 19.6 us  [exchange(): return lax.all_to_all(parts, axes, 0, 0, tiled=True)]
    ppermute x3, waiting for transfers between devices: 0.01 us -> 2.08 us  [around(): b = lax.ppermute(b, axis, down)]
    ppermute x3, starting transfers between devices: 15 us -> 12.9 us  [around(): b = lax.ppermute(b, axis, down)]
  transfers between devices with their start and end apart: 16 -> 16, of which waited for: 7 -> 9; matrix products, arithmetic and copies ran while one was open for 0% -> 1% of each run, Pallas kernels for 3% -> 3%
where the time goes in v4:
time: 184 us; the launch traced here: 183 us
  starting transfers between devices  66.7 us (36%)
  blocking collectives  65.2 us (35%)
  waiting for transfers between devices  37 us (20%)
  Pallas kernels  8.05 us (4%)
  local copies, waits for them, and re-layouts  3.37 us (2%)
    all_to_all x2, blocking collectives, exchange(): return lax.all_to_all(parts, axes, 0, 0, tiled=True)  65.2 us
    all_to_all x3, waiting for transfers between devices, exchange(): return lax.all_to_all(parts, axes, 0, 0, tiled=True)  22 us
    all_to_all x3, starting transfers between devices, exchange(): return lax.all_to_all(parts, axes, 0, 0, tiled=True)  19.6 us
    ppermute x4, starting transfers between devices, per_device(): blocks[k - 1] = lax.ppermute(blocks[k - 1], ('y', 'dp'), pairs)  13.6 us
    ppermute x3, starting transfers between devices, around(): b = lax.ppermute(b, axis, down)  12.9 us
    ppermute x4, starting transfers between devices, around(): a = lax.ppermute(a, axis, up)  8.25 us
    ppermute x1, starting transfers between devices, per_device(): other = lax.ppermute(mine, 'core', [(0, 1), (1, 0)])  7.53 us
    ppermute x4, waiting for transfers between devices, around(): a = lax.ppermute(a, axis, up)  6.96 us
  transfers between devices with their start and end apart: 16, of which 9 were waited for; matrix products, arithmetic and copies ran while one was open for 1% of the time, Pallas kernels for 3%

profile of v4, /device:TPU:1, one launch (start us, length us, event | category | flops | bytes accessed | tf_op | source)
XLA Modules:
  0.0 182.8 jit_solution(18122034679059209506)
XLA Ops:
  0.0 0.8 copy-done.2
  0.8 0.7 in_columns.1
  1.5 10.2 %all-to-all-start = ((bf16[16,4,896]{2,1,0:T(4,128)(2,1)}), bf16[16,4,896]{2,1,0:T(4,128)(2,1)S(1)}, u32[]{:S(2)}, u32[]{:S(2)}) async-start(bf16[16,4,896]{2,1,0:T(4,128)(2,1)} %in_columns.1), calls=%async_computation | async-start | bytes 229376 | tf_op jit(solution)/shard_map/all_to_all | solution.py:17
  11.7 0.7 fusion.4
  12.4 0.2 convolution_bitcast_fusion.2
  12.6 8.9 %all-to-all-done = bf16[16,4,896]{2,1,0:T(4,128)(2,1)S(1)} async-done(((bf16[16,4,896]{2,1,0:T(4,128)(2,1)}), bf16[16,4,896]{2,1,0:T(4,128)(2,1)S(1)}, u32[]{:S(2)}, u32[]{:S(2)}) %all-to-all-start) | async-done | bytes 114720 | tf_op jit(solution)/shard_map/all_to_all | solution.py:17
  21.5 0.2 convolution_convert_fusion
  21.9 41.1 %all_to_all.25 = bf16[32,4,896]{2,1,0:T(4,128)(2,1)S(1)} all-to-all(bf16[32,4,896]{2,1,0:T(4,128)(2,1)S(1)} %copy.24), channel_id=1, replica_groups=mesh['y'=8,'xh'=2,'z'=16,'core'=2,'dp'=2] {'z','core'}, dimensions={0} | all-to-all | bytes 458752 | tf_op jit(solution)/shard_map/all_to_all | solution.py:17
  63.1 2.3 %collective-permute-start = (bf16[128,896]{1,0:T(8,128)(2,1)S(1)}, bf16[128,896]{1,0:T(8,128)(2,1)S(1)}, u32[]{:S(2)}, u32[]{:S(2)}) collective-permute-start(bf16[128,896]{1,0:T(8,128)(2,1)S(1)} %reshape.64.refs_0_), channel_id=1, source_target_pairs={{0,128},{128,256},{256,384},{384,512},{512,640},{640,768},{768,896... | collective-permute-start | bytes 688136 | tf_op jit(solution)/shard_map/ppermute | solution.py:206
  65.4 4.4 %collective-permute-start.4 = (bf16[128,896]{1,0:T(8,128)(2,1)S(1)}, bf16[128,896]{1,0:T(8,128)(2,1)S(1)}, u32[]{:S(2)}, u32[]{:S(2)}) collective-permute-start(bf16[128,896]{1,0:T(8,128)(2,1)S(1)} %reshape.64.refs_0_), channel_id=1, source_target_pairs={{0,896},{128,0},{256,128},{384,256},{512,384},{640,512},{768,640},... | collective-permute-start | bytes 688136 | tf_op jit(solution)/shard_map/ppermute | solution.py:209
  69.8 2.4 %collective-permute-done.refs_0_ = bf16[128,896]{1,0:T(8,128)(2,1)S(1)} collective-permute-done((bf16[128,896]{1,0:T(8,128)(2,1)S(1)}, bf16[128,896]{1,0:T(8,128)(2,1)S(1)}, u32[]{:S(2)}, u32[]{:S(2)}) %collective-permute-start) | collective-permute-done | bytes 229408 | tf_op jit(solution)/shard_map/ppermute | solution.py:206
  72.3 1.9 %collective-permute-start.1 = (bf16[128,896]{1,0:T(8,128)(2,1)S(1)}, bf16[128,896]{1,0:T(8,128)(2,1)S(1)}, u32[]{:S(2)}, u32[]{:S(2)}) collective-permute-start(bf16[128,896]{1,0:T(8,128)(2,1)S(1)} %collective-permute-done.refs_0_), channel_id=1, source_target_pairs={{0,128},{128,256},{256,384},{384,512},{512,640},{640,768},{768,896... | collective-permute-start | bytes 688136 | tf_op jit(solution)/shard_map/ppermute | solution.py:206
  74.2 1.4 cut_blocks.1
  75.6 2.4 %collective-permute-start.10 = (bf16[64,896]{1,0:T(8,128)(2,1)S(1)}, bf16[64,896]{1,0:T(8,128)(2,1)S(1)}, u32[]{:S(2)}, u32[]{:S(2)}) collective-permute-start(bf16[64,896]{1,0:T(8,128)(2,1)S(1)} %get-tuple-element.42), channel_id=1, source_target_pairs={{0,512},{1,513},{128,640},{129,641},{256,768},{257,769},{384,896},... | collective-permute-start | bytes 344072 | tf_op jit(solution)/shard_map/ppermute | solution.py:233
  78.0 3.0 %collective-permute-start.7 = (bf16[128,896]{1,0:T(8,128)(2,1)S(1)}, bf16[128,896]{1,0:T(8,128)(2,1)S(1)}, u32[]{:S(2)}, u32[]{:S(2)}) collective-permute-start(bf16[128,896]{1,0:T(8,128)(2,1)S(1)} %get-tuple-element.39), channel_id=1, source_target_pairs={{0,128},{1,897},{128,256},{129,1},{256,384},{257,129},{384,512},{3... | collective-permute-start | bytes 688136 | tf_op jit(solution)/shard_map/ppermute | solution.py:233
  81.0 6.3 %collective-permute-start.8 = (bf16[128,896]{1,0:T(8,128)(2,1)S(1)}, bf16[128,896]{1,0:T(8,128)(2,1)S(1)}, u32[]{:S(2)}, u32[]{:S(2)}) collective-permute-start(bf16[128,896]{1,0:T(8,128)(2,1)S(1)} %get-tuple-element.40), channel_id=1, source_target_pairs={{0,256},{1,769},{128,384},{129,897},{256,512},{257,1},{384,640},{3... | collective-permute-start | bytes 688136 | tf_op jit(solution)/shard_map/ppermute | solution.py:233
  87.3 1.9 %collective-permute-start.9 = (bf16[128,896]{1,0:T(8,128)(2,1)S(1)}, bf16[128,896]{1,0:T(8,128)(2,1)S(1)}, u32[]{:S(2)}, u32[]{:S(2)}) collective-permute-start(bf16[128,896]{1,0:T(8,128)(2,1)S(1)} %get-tuple-element.41), channel_id=1, source_target_pairs={{0,640},{1,385},{128,768},{129,513},{256,896},{257,641},{384,0},{3... | collective-permute-start | bytes 688136 | tf_op jit(solution)/shard_map/ppermute | solution.py:233
  89.2 3.2 %collective-permute-start.5 = (bf16[128,896]{1,0:T(8,128)(2,1)S(1)}, bf16[128,896]{1,0:T(8,128)(2,1)S(1)}, u32[]{:S(2)}, u32[]{:S(2)}) collective-permute-start(bf16[128,896]{1,0:T(8,128)(2,1)S(1)} %collective-permute-done.4.refs_0_), channel_id=1, source_target_pairs={{0,896},{128,0},{256,128},{384,256},{512,384},{640,512},{768,640},... | collective-permute-start | bytes 688136 | tf_op jit(solution)/shard_map/ppermute | solution.py:209
  92.4 2.1 %collective-permute-start.2 = (bf16[128,896]{1,0:T(8,128)(2,1)S(1)}, bf16[128,896]{1,0:T(8,128)(2,1)S(1)}, u32[]{:S(2)}, u32[]{:S(2)}) collective-permute-start(bf16[128,896]{1,0:T(8,128)(2,1)S(1)} %collective-permute-done.1.refs_0_), channel_id=1, source_target_pairs={{0,128},{128,256},{256,384},{384,512},{512,640},{640,768},{768,896... | collective-permute-start | bytes 688136 | tf_op jit(solution)/shard_map/ppermute | solution.py:206
  94.5 3.2 %collective-permute-done.8.refs_1_ = bf16[128,896]{1,0:T(8,128)(2,1)S(1)} collective-permute-done((bf16[128,896]{1,0:T(8,128)(2,1)S(1)}, bf16[128,896]{1,0:T(8,128)(2,1)S(1)}, u32[]{:S(2)}, u32[]{:S(2)}) %collective-permute-start.8) | collective-permute-done | bytes 229408 | tf_op jit(solution)/shard_map/ppermute | solution.py:233
  97.8 2.0 %collective-permute-done.9.refs_2_ = bf16[128,896]{1,0:T(8,128)(2,1)S(1)} collective-permute-done((bf16[128,896]{1,0:T(8,128)(2,1)S(1)}, bf16[128,896]{1,0:T(8,128)(2,1)S(1)}, u32[]{:S(2)}, u32[]{:S(2)}) %collective-permute-start.9) | collective-permute-done | bytes 229408 | tf_op jit(solution)/shard_map/ppermute | solution.py:233
  99.7 0.7 copy-done.5
  100.4 1.3 stacked.1.mine_ref
  101.7 4.8 %collective-permute-start.11 = (bf16[448,896]{1,0:T(8,128)(2,1)S(1)}, bf16[448,896]{1,0:T(8,128)(2,1)}, u32[]{:S(2)}, u32[]{:S(2)}) collective-permute-start(bf16[448,896]{1,0:T(8,128)(2,1)S(1)} %stacked.1.mine_ref), channel_id=1, source_target_pairs={{0,1},{1,0},{2,3},{3,2},{4,5},{5,4},{6,7},{7,6},{8,9},{9,8},{10,11... | collective-permute-start | bytes 2408456 | tf_op jit(solution)/shard_map/ppermute | solution.py:235
  106.5 2.1 %collective-permute-done.5.refs_0_ = bf16[128,896]{1,0:T(8,128)(2,1)S(1)} collective-permute-done((bf16[128,896]{1,0:T(8,128)(2,1)S(1)}, bf16[128,896]{1,0:T(8,128)(2,1)S(1)}, u32[]{:S(2)}, u32[]{:S(2)}) %collective-permute-start.5) | collective-permute-done | bytes 229408 | tf_op jit(solution)/shard_map/ppermute | solution.py:209
  108.6 5.3 %collective-permute-start.6 = (bf16[128,896]{1,0:T(8,128)(2,1)S(1)}, bf16[128,896]{1,0:T(8,128)(2,1)S(1)}, u32[]{:S(2)}, u32[]{:S(2)}) collective-permute-start(bf16[128,896]{1,0:T(8,128)(2,1)S(1)} %collective-permute-done.5.refs_0_), channel_id=1, source_target_pairs={{0,896},{128,0},{256,128},{384,256},{512,384},{640,512},{768,640},... | collective-permute-start | bytes 688136 | tf_op jit(solution)/shard_map/ppermute | solution.py:209
  113.9 1.9 %collective-permute-start.3 = (bf16[128,896]{1,0:T(8,128)(2,1)S(1)}, bf16[128,896]{1,0:T(8,128)(2,1)S(1)}, u32[]{:S(2)}, u32[]{:S(2)}) collective-permute-start(bf16[128,896]{1,0:T(8,128)(2,1)S(1)} %collective-permute-done.2.refs_0_), channel_id=1, source_target_pairs={{0,128},{128,256},{256,384},{384,512},{512,640},{640,768},{768,896... | collective-permute-start | bytes 688136 | tf_op jit(solution)/shard_map/ppermute | solution.py:206
  115.9 0.3 gate_up_step.8
  116.2 0.3 gate_up_step.9
  116.5 0.3 gate_up_step.10
  116.7 0.3 gate_up_step.11
  117.0 0.3 gate_up_step.12
  117.3 0.3 gate_up_step.13
  117.6 0.3 gate_up_step.14
  117.9 4.5 %collective-permute-done.3.refs_0_ = bf16[128,896]{1,0:T(8,128)(2,1)S(1)} collective-permute-done((bf16[128,896]{1,0:T(8,128)(2,1)S(1)}, bf16[128,896]{1,0:T(8,128)(2,1)S(1)}, u32[]{:S(2)}, u32[]{:S(2)}) %collective-permute-start.3) | collective-permute-done | bytes 229408 | tf_op jit(solution)/shard_map/ppermute | solution.py:206
  122.5 1.0 gate_up_step.15
  123.5 4.6 %all-to-all-start.2 = ((bf16[8,128,128]{2,1,0:T(8,128)(2,1)}), bf16[8,128,128]{2,1,0:T(8,128)(2,1)S(1)}, u32[]{:S(2)}, u32[]{:S(2)}) async-start(bf16[8,128,128]{2,1,0:T(8,128)(2,1)} %gate_up_step.15), calls=%async_computation.2 | async-start | bytes 524288 | tf_op jit(solution)/shard_map/all_to_all | solution.py:17
  128.1 7.5 %collective-permute-start.12 = (s32[2,64,8]{1,2,0:T(8,128)S(1)}, s32[2,64,8]{1,2,0:T(8,128)S(1)}, u32[]{:S(2)}, u32[]{:S(2)}) collective-permute-start(s32[2,64,8]{1,2,0:T(8,128)S(1)} %constant_dynamic-update-slice_fusion), channel_id=1, source_target_pairs={{0,2},{2,0},{1,3},{3,1},{4,6},{6,4},{5,7},{7,5},{8,10},{10,8},{9,1... | collective-permute-start | bytes 12296 | tf_op jit(solution)/shard_map/ppermute | solution.py:222
  135.7 0.8 collective-permute-done.12
  136.5 0.9 all-to-all-done.2.hid_ref
  137.4 1.8 down_product.1
  139.2 0.8 reshape.65
  139.9 4.8 %all-to-all-start.3 = ((bf16[16,2,4,896]{3,2,1,0:T(4,128)(2,1)}), bf16[16,2,4,896]{3,2,1,0:T(4,128)(2,1)S(1)}, u32[]{:S(2)}, u32[]{:S(2)}) async-start(bf16[16,2,4,896]{3,2,1,0:T(4,128)(2,1)} %reshape.65), calls=%async_computation.3 | async-start | bytes 458752 | tf_op jit(solution)/shard_map/all_to_all | solution.py:17
  144.9 0.2 convolution_bitcast_fusion.1
  145.1 12.2 %all-to-all-done.3 = bf16[16,2,4,896]{3,2,1,0:T(4,128)(2,1)S(1)} async-done(((bf16[16,2,4,896]{3,2,1,0:T(4,128)(2,1)}), bf16[16,2,4,896]{3,2,1,0:T(4,128)(2,1)S(1)}, u32[]{:S(2)}, u32[]{:S(2)}) %all-to-all-start.3) | async-done | bytes 229408 | tf_op jit(solution)/shard_map/all_to_all | solution.py:17
  157.3 0.4 fusion.1
  157.9 24.0 %all_to_all.26 = bf16[32,4,896]{2,1,0:T(4,128)(2,1)S(1)} all-to-all(bf16[32,4,896]{2,1,0:T(4,128)(2,1)S(1)} %bitcast.92), channel_id=1, replica_groups=mesh['y'=8,'xh'=2,'z'=16,'core'=2,'dp'=2] {'y','xh','core'}, dimensions={0} | all-to-all | bytes 458752 | tf_op jit(solution)/shard_map/all_to_all | solution.py:17
  182.2 0.6 copy-done.9
  (48 shorter events, 0.8 us)
Async XLA Ops:
  0.0 0.8 copy-start.2
  1.5 20.0 %all-to-all-start = ((bf16[16,4,896]{2,1,0:T(4,128)(2,1)}), bf16[16,4,896]{2,1,0:T(4,128)(2,1)S(1)}, u32[]{:S(2)}, u32[]{:S(2)}) async-start(bf16[16,4,896]{2,1,0:T(4,128)(2,1)} %in_columns.1), calls=%async_computation | async-start | bytes 229376 | tf_op jit(solution)/shard_map/all_to_all | solution.py:17
  63.0 52.9 %copy-start.1 = (bf16[1,7168,128]{2,1,0:T(8,128)(2,1)S(1)}, bf16[1,7168,128]{2,1,0:T(8,128)(2,1)}, u32[]{:S(2)}) copy-start(bf16[1,7168,128]{2,1,0:T(8,128)(2,1)} %param.10) | copy-start | bytes 5505028
  63.1 52.8 %copy-start = (bf16[1,7168,128]{2,1,0:T(8,128)(2,1)S(1)}, bf16[1,7168,128]{2,1,0:T(8,128)(2,1)}, u32[]{:S(2)}) copy-start(bf16[1,7168,128]{2,1,0:T(8,128)(2,1)} %param.9) | copy-start | bytes 5505028
  63.1 9.2 %collective-permute-start = (bf16[128,896]{1,0:T(8,128)(2,1)S(1)}, bf16[128,896]{1,0:T(8,128)(2,1)S(1)}, u32[]{:S(2)}, u32[]{:S(2)}) collective-permute-start(bf16[128,896]{1,0:T(8,128)(2,1)S(1)} %reshape.64.refs_0_), channel_id=1, source_target_pairs={{0,128},{128,256},{256,384},{384,512},{512,640},{640,768},{768,896... | collective-permute-start | bytes 688136 | tf_op jit(solution)/shard_map/ppermute | solution.py:206
  65.4 23.8 %collective-permute-start.4 = (bf16[128,896]{1,0:T(8,128)(2,1)S(1)}, bf16[128,896]{1,0:T(8,128)(2,1)S(1)}, u32[]{:S(2)}, u32[]{:S(2)}) collective-permute-start(bf16[128,896]{1,0:T(8,128)(2,1)S(1)} %reshape.64.refs_0_), channel_id=1, source_target_pairs={{0,896},{128,0},{256,128},{384,256},{512,384},{640,512},{768,640},... | collective-permute-start | bytes 688136 | tf_op jit(solution)/shard_map/ppermute | solution.py:209
  72.3 20.1 %collective-permute-start.1 = (bf16[128,896]{1,0:T(8,128)(2,1)S(1)}, bf16[128,896]{1,0:T(8,128)(2,1)S(1)}, u32[]{:S(2)}, u32[]{:S(2)}) collective-permute-start(bf16[128,896]{1,0:T(8,128)(2,1)S(1)} %collective-permute-done.refs_0_), channel_id=1, source_target_pairs={{0,128},{128,256},{256,384},{384,512},{512,640},{640,768},{768,896... | collective-permute-start | bytes 688136 | tf_op jit(solution)/shard_map/ppermute | solution.py:206
  75.6 11.7 %collective-permute-start.10 = (bf16[64,896]{1,0:T(8,128)(2,1)S(1)}, bf16[64,896]{1,0:T(8,128)(2,1)S(1)}, u32[]{:S(2)}, u32[]{:S(2)}) collective-permute-start(bf16[64,896]{1,0:T(8,128)(2,1)S(1)} %get-tuple-element.42), channel_id=1, source_target_pairs={{0,512},{1,513},{128,640},{129,641},{256,768},{257,769},{384,896},... | collective-permute-start | bytes 344072 | tf_op jit(solution)/shard_map/ppermute | solution.py:233
  78.0 16.5 %collective-permute-start.7 = (bf16[128,896]{1,0:T(8,128)(2,1)S(1)}, bf16[128,896]{1,0:T(8,128)(2,1)S(1)}, u32[]{:S(2)}, u32[]{:S(2)}) collective-permute-start(bf16[128,896]{1,0:T(8,128)(2,1)S(1)} %get-tuple-element.39), channel_id=1, source_target_pairs={{0,128},{1,897},{128,256},{129,1},{256,384},{257,129},{384,512},{3... | collective-permute-start | bytes 688136 | tf_op jit(solution)/shard_map/ppermute | solution.py:233
  81.0 16.8 %collective-permute-start.8 = (bf16[128,896]{1,0:T(8,128)(2,1)S(1)}, bf16[128,896]{1,0:T(8,128)(2,1)S(1)}, u32[]{:S(2)}, u32[]{:S(2)}) collective-permute-start(bf16[128,896]{1,0:T(8,128)(2,1)S(1)} %get-tuple-element.40), channel_id=1, source_target_pairs={{0,256},{1,769},{128,384},{129,897},{256,512},{257,1},{384,640},{3... | collective-permute-start | bytes 688136 | tf_op jit(solution)/shard_map/ppermute | solution.py:233
  87.3 12.5 %copy-start.6 = (bf16[64,896]{1,0:T(8,128)(2,1)}, bf16[64,896]{1,0:T(8,128)(2,1)S(1)}, u32[]{:S(2)}) copy-start(bf16[64,896]{1,0:T(8,128)(2,1)S(1)} %collective-permute-done.10.refs_3_) | copy-start | bytes 344068
  87.3 12.5 %collective-permute-start.9 = (bf16[128,896]{1,0:T(8,128)(2,1)S(1)}, bf16[128,896]{1,0:T(8,128)(2,1)S(1)}, u32[]{:S(2)}, u32[]{:S(2)}) collective-permute-start(bf16[128,896]{1,0:T(8,128)(2,1)S(1)} %get-tuple-element.41), channel_id=1, source_target_pairs={{0,640},{1,385},{128,768},{129,513},{256,896},{257,641},{384,0},{3... | collective-permute-start | bytes 688136 | tf_op jit(solution)/shard_map/ppermute | solution.py:233
  89.2 19.4 %collective-permute-start.5 = (bf16[128,896]{1,0:T(8,128)(2,1)S(1)}, bf16[128,896]{1,0:T(8,128)(2,1)S(1)}, u32[]{:S(2)}, u32[]{:S(2)}) collective-permute-start(bf16[128,896]{1,0:T(8,128)(2,1)S(1)} %collective-permute-done.4.refs_0_), channel_id=1, source_target_pairs={{0,896},{128,0},{256,128},{384,256},{512,384},{640,512},{768,640},... | collective-permute-start | bytes 688136 | tf_op jit(solution)/shard_map/ppermute | solution.py:209
  92.4 21.5 %collective-permute-start.2 = (bf16[128,896]{1,0:T(8,128)(2,1)S(1)}, bf16[128,896]{1,0:T(8,128)(2,1)S(1)}, u32[]{:S(2)}, u32[]{:S(2)}) collective-permute-start(bf16[128,896]{1,0:T(8,128)(2,1)S(1)} %collective-permute-done.1.refs_0_), channel_id=1, source_target_pairs={{0,128},{128,256},{256,384},{384,512},{512,640},{640,768},{768,896... | collective-permute-start | bytes 688136 | tf_op jit(solution)/shard_map/ppermute | solution.py:206
  94.5 5.2 %copy-start.3 = (bf16[128,896]{1,0:T(8,128)(2,1)}, bf16[128,896]{1,0:T(8,128)(2,1)S(1)}, u32[]{:S(2)}) copy-start(bf16[128,896]{1,0:T(8,128)(2,1)S(1)} %collective-permute-done.7.refs_0_) | copy-start | bytes 688132
  97.8 2.0 %copy-start.4 = (bf16[128,896]{1,0:T(8,128)(2,1)}, bf16[128,896]{1,0:T(8,128)(2,1)S(1)}, u32[]{:S(2)}) copy-start(bf16[128,896]{1,0:T(8,128)(2,1)S(1)} %collective-permute-done.8.refs_1_) | copy-start | bytes 688132
  99.7 0.7 copy-start.5
  101.7 34.8 %collective-permute-start.11 = (bf16[448,896]{1,0:T(8,128)(2,1)S(1)}, bf16[448,896]{1,0:T(8,128)(2,1)}, u32[]{:S(2)}, u32[]{:S(2)}) collective-permute-start(bf16[448,896]{1,0:T(8,128)(2,1)S(1)} %stacked.1.mine_ref), channel_id=1, source_target_pairs={{0,1},{1,0},{2,3},{3,2},{4,5},{5,4},{6,7},{7,6},{8,9},{9,8},{10,11... | collective-permute-start | bytes 2408456 | tf_op jit(solution)/shard_map/ppermute | solution.py:235
  108.6 9.0 %collective-permute-start.6 = (bf16[128,896]{1,0:T(8,128)(2,1)S(1)}, bf16[128,896]{1,0:T(8,128)(2,1)S(1)}, u32[]{:S(2)}, u32[]{:S(2)}) collective-permute-start(bf16[128,896]{1,0:T(8,128)(2,1)S(1)} %collective-permute-done.5.refs_0_), channel_id=1, source_target_pairs={{0,896},{128,0},{256,128},{384,256},{512,384},{640,512},{768,640},... | collective-permute-start | bytes 688136 | tf_op jit(solution)/shard_map/ppermute | solution.py:209
  113.9 8.6 %collective-permute-start.3 = (bf16[128,896]{1,0:T(8,128)(2,1)S(1)}, bf16[128,896]{1,0:T(8,128)(2,1)S(1)}, u32[]{:S(2)}, u32[]{:S(2)}) collective-permute-start(bf16[128,896]{1,0:T(8,128)(2,1)S(1)} %collective-permute-done.2.refs_0_), channel_id=1, source_target_pairs={{0,128},{128,256},{256,384},{384,512},{512,640},{640,768},{768,896... | collective-permute-start | bytes 688136 | tf_op jit(solution)/shard_map/ppermute | solution.py:206
  122.5 5.6 %copy-start.7 = (s32[1,64,8]{1,2,0:T(8,128)S(1)}, s32[1,64,8]{1,2,0:T(8,128)}, u32[]{:S(2)}) copy-start(s32[1,64,8]{1,2,0:T(8,128)} %param.7) | copy-start | bytes 6148
  122.5 5.6 %copy-start.8 = (s32[1,64,8]{1,2,0:T(8,128)S(1)}, s32[1,64,8]{1,2,0:T(8,128)}, u32[]{:S(2)}) copy-start(s32[1,64,8]{1,2,0:T(8,128)} %param.8) | copy-start | bytes 6148
  123.5 13.9 %all-to-all-start.2 = ((bf16[8,128,128]{2,1,0:T(8,128)(2,1)}), bf16[8,128,128]{2,1,0:T(8,128)(2,1)S(1)}, u32[]{:S(2)}, u32[]{:S(2)}) async-start(bf16[8,128,128]{2,1,0:T(8,128)(2,1)} %gate_up_step.15), calls=%async_computation.2 | async-start | bytes 524288 | tf_op jit(solution)/shard_map/all_to_all | solution.py:17
  128.1 8.3 %collective-permute-start.12 = (s32[2,64,8]{1,2,0:T(8,128)S(1)}, s32[2,64,8]{1,2,0:T(8,128)S(1)}, u32[]{:S(2)}, u32[]{:S(2)}) collective-permute-start(s32[2,64,8]{1,2,0:T(8,128)S(1)} %constant_dynamic-update-slice_fusion), channel_id=1, source_target_pairs={{0,2},{2,0},{1,3},{3,1},{4,6},{6,4},{5,7},{7,5},{8,10},{10,8},{9,1... | collective-permute-start | bytes 12296 | tf_op jit(solution)/shard_map/ppermute | solution.py:222
  139.9 17.4 %all-to-all-start.3 = ((bf16[16,2,4,896]{3,2,1,0:T(4,128)(2,1)}), bf16[16,2,4,896]{3,2,1,0:T(4,128)(2,1)S(1)}, u32[]{:S(2)}, u32[]{:S(2)}) async-start(bf16[16,2,4,896]{3,2,1,0:T(4,128)(2,1)} %reshape.65), calls=%async_computation.3 | async-start | bytes 458752 | tf_op jit(solution)/shard_map/all_to_all | solution.py:17
  182.2 0.6 copy-start.9
